TPU v7x, 256 devices: a whole 4x4x8 slice. The times are simulated.
256 devices in a mesh: tp: 64 (over y, x, z_hi), col: 4 (over z_lo, core).
Axes of the slice: x: 4, y: 4, z: 8 (z_hi: 4, z_lo: 2; z = z_hi * 2 + z_lo), core: 2. Of those that a mesh axis runs over, the one named last changes fastest.
Arguments:
- gate_in: bfloat16 [1024, 53248], P('col', 'tp'), may hold values from -6 to 6
- up_in: bfloat16 [1024, 53248], P('col', 'tp'), may hold values from -6 to 6
- down_weight: bfloat16 [53248, 16384], P('tp', 'col'), may hold values from -0.02734375 to 0.02734375
- residual: bfloat16 [1024, 16384], P('tp', 'col'), may hold values from -30 to 30
- norm_gain: bfloat16 [16384], P('col'), may hold values from 0.5 to 1.5
Outputs:
- stream: bfloat16 [1024, 16384], P('tp', 'col')
- normed: bfloat16 [1024, 16384], P('tp', 'col')
All inputs are finite; a program needn't handle non-finite values.
Results may differ from a plain program's by a relative error of at most 0.0034.
Values may be sent and summed in bfloat16 or wider, within the bound.
A program may use at most 128 MiB of HBM per device.

v0:
```python
import jax
import jax.numpy as jnp
from jax import lax
from jax.sharding import Mesh
from jax.sharding import PartitionSpec as P

D = 16384
TP = ("tp_0", "tp_1", "tp_2")


def joined_along(tiles, dim):
    lengths = list(tiles.shape[1:])
    lengths[dim] *= tiles.shape[0]
    return jnp.moveaxis(tiles, 0, dim).reshape(lengths)


def from_everyone(value, axis):
    peers = lax.axis_size(axis)
    return lax.all_to_all(
        jnp.broadcast_to(value[None], (peers, *value.shape)), axis, 0, 0, tiled=True
    )


def gather_directly(value, axis, dim):
    return joined_along(from_everyone(value, axis), dim)


def summed_rows(value, axes, dim):
    if not axes:
        return value
    nearer = lax.psum_scatter(value, axes[0], scatter_dimension=dim, tiled=True)
    return summed_rows(nearer, axes[1:], dim)


def total_of_pieces(value, axis):
    tiles = lax.all_gather(value, axis)
    return tiles.sum(axis=0)


def gated(gate_part, up_part):
    return (jax.nn.silu(gate_part.astype(jnp.float32)) * up_part.astype(jnp.float32)).astype(
        jnp.bfloat16
    )


def body(gate_in, up_in, down_weight, residual, norm_gain):
    local_act = gated(gate_in, up_in)
    hidden = gather_directly(local_act, "col", 0)
    partial_value = jnp.dot(hidden, down_weight, preferred_element_type=jnp.float32)
    branch = summed_rows(partial_value, TP, 0)
    summed = residual.astype(jnp.float32) + branch
    local_squares = jnp.sum(summed * summed, axis=1, keepdims=True)
    mean_square = total_of_pieces(local_squares, "col") / D
    scaled = summed * lax.rsqrt(mean_square + 1e-05) * norm_gain.astype(jnp.float32)[None, :]
    return (summed.astype(jnp.bfloat16), scaled.astype(jnp.bfloat16))


def solution(mesh):
    split = Mesh(mesh.devices.reshape(4, 4, 4, mesh.shape["col"]), ("tp_0", "tp_1", "tp_2", "col"))
    return jax.shard_map(
        body,
        mesh=split,
        in_specs=(P("col", TP), P("col", TP), P(TP, "col"), P(TP, "col"), P("col")),
        out_specs=(P(TP, "col"), P(TP, "col")),
        check_vma=False,
    )
```

profile of v0, /device:TPU:1, one launch (start us, length us, event | category | flops | bytes accessed | tf_op | source)
XLA Modules:
  0.0 302.4 jit_solution(8682976006773111219)
XLA Ops:
  7.2 0.0 reduce-scatter.4.cloned.1.call-start
  7.2 1.4 fusion.4
  8.6 0.0 copy-start.2
  8.6 0.1 broadcast_in_dim.2
  8.8 26.5 %all_to_all.5 = bf16[4,256,832]{1,2,0:T(8,128)(2,1)S(1)} all-to-all(bf16[4,256,832]{1,2,0:T(8,128)(2,1)S(1)} %broadcast_in_dim.2), channel_id=1, replica_groups=mesh['tp_0'=4,'tp_1'=4,'tp_2'=4,'col'=4] {'col'}, dimensions={0} | all-to-all | bytes 3407872 | tf_op jit(solution)/shard_map/all_to_all | solution.py:19
  35.2 0.2 copy.9
  35.4 0.0 copy-done.2
  35.5 11.6 %fusion.6 = f32[1024,4096]{1,0:T(8,128)} fusion(bf16[1024,832]{0,1:T(8,128)(2,1)S(1)} %bitcast.6, bf16[832,4096]{1,0:T(8,128)(2,1)S(1)} %copy-done.2), kind=kOutput, calls=%fused_computation.12 | convolution fusion | flops 6979321856 | bytes 25296896 | tf_op jit(solution)/shard_map/dot_general | solution.py:49
  47.0 0.0 reduce-scatter.4.cloned.1.call-update
  47.0 0.0 copy-start.1
  47.1 0.0 copy-start.3
  47.1 0.0 copy-start
  47.1 0.0 reduce-scatter.6.cloned.1.call-start
  47.1 152.2 %reduce-scatter.4.cloned.1.call-done = f32[256,4096]{1,0:T(8,128)} async-done(((f32[1024,4096]{1,0:T(8,128)}), f32[256,4096]{1,0:T(8,128)}) %reduce-scatter.4.cloned.1.call-update) | async-done | bytes 4194320 | tf_op jit(solution)/shard_map/reduce_scatter | solution.py:31
  199.3 0.0 reduce-scatter.6.cloned.1.call-update
  199.3 0.0 reduce-scatter.8.cloned.1.call-start
  199.4 51.6 %reduce-scatter.6.cloned.1.call-done = f32[64,4096]{1,0:T(8,128)} async-done(((f32[256,4096]{1,0:T(8,128)}), f32[64,4096]{1,0:T(8,128)}) %reduce-scatter.6.cloned.1.call-update) | async-done | bytes 1048592 | tf_op jit(solution)/shard_map/reduce_scatter | solution.py:31
  251.0 0.0 reduce-scatter.8.cloned.1.call-update
  251.0 0.0 copy-done.1
  251.0 0.0 copy-done.3
  251.0 0.6 dynamic-slice
  252.3 33.7 %reduce-scatter.8.cloned.1.call-done = f32[16,4096]{1,0:T(8,128)} async-done(((f32[64,4096]{1,0:T(8,128)}), f32[16,4096]{1,0:T(8,128)}) %reduce-scatter.8.cloned.1.call-update) | async-done | bytes 262160 | tf_op jit(solution)/shard_map/reduce_scatter | solution.py:31
  286.0 0.0 copy-done
  286.0 1.1 multiply_reduce_fusion
  287.1 0.2 dynamic-update-slice
  287.3 6.8 %all-reduce = f32[64]{0:T(128)S(1)} all-reduce(f32[64]{0:T(128)S(1)} %dynamic-update-slice), channel_id=2, replica_groups=mesh['tp_0'=4,'tp_1'=4,'tp_2'=4,'col'=4] {'col'}, use_global_device_ids=true, to_apply=%add | all-reduce | flops 64 | bytes 512
  294.1 0.1 reshape.19
  294.2 1.7 multiply_convert_fusion
  (4 shorter events, 0.0 us)
Async XLA Ops:
  7.2 192.1 %reduce-scatter.4.cloned.1.call-start = ((), (), s32[]{:S(2)}) async-start(), calls=%async_computation.4 | async-start | bytes 20971520 | tf_op jit(solution)/shard_map/reduce_scatter | solution.py:31
  8.6 26.8 %copy-start.2 = (bf16[832,4096]{1,0:T(8,128)(2,1)S(1)}, bf16[832,4096]{1,0:T(8,128)(2,1)}, u32[]{:S(2)}) copy-start(bf16[832,4096]{1,0:T(8,128)(2,1)} %param.7) | copy-start | bytes 20447236
  47.0 203.9 %copy-start.1 = (bf16[4096]{0:T(1024)(128)(2,1)S(1)}, bf16[4096]{0:T(1024)(128)(2,1)}, u32[]{:S(2)}) copy-start(bf16[4096]{0:T(1024)(128)(2,1)} %param.9) | copy-start | bytes 24580
  47.1 204.0 %copy-start.3 = (u32[256]{0:T(256)S(1)}, u32[256]{0:T(256)}, u32[]{:S(2)}) copy-start(u32[256]{0:T(256)} %constant.13) | copy-start | bytes 3076
  47.1 238.9 %copy-start = (bf16[16,4096]{1,0:T(8,128)(2,1)S(1)}, bf16[16,4096]{1,0:T(8,128)(2,1)}, u32[]{:S(2)}) copy-start(bf16[16,4096]{1,0:T(8,128)(2,1)} %param.8) | copy-start | bytes 393220
  47.1 203.9 %reduce-scatter.6.cloned.1.call-start = ((), (), s32[]{:S(2)}) async-start(), calls=%async_computation.5 | async-start | bytes 5242880 | tf_op jit(solution)/shard_map/reduce_scatter | solution.py:31
  199.3 86.6 %reduce-scatter.8.cloned.1.call-start = ((), (), s32[]{:S(2)}) async-start(), calls=%async_computation.6 | async-start | bytes 1310720 | tf_op jit(solution)/shard_map/reduce_scatter | solution.py:31
Sparse Core Ops, SparseCore 0:
  47.2 152.0 reduce-scatter.3
  201.8 49.0 reduce-scatter.5
  253.5 32.3 reduce-scatter.7
where the time goes:
time: 303 us; the launch traced here: 302 us
  waiting for transfers between devices  237 us (78%)
  blocking collectives  33.2 us (11%)
  between operations  14.5 us (5%)
  matrix products  11.6 us (4%)
  other arithmetic  4.24 us (1%)
    reduce_scatter x3, waiting for transfers between devices, summed_rows(): nearer = lax.psum_scatter(value, axes[0], scatter_dimension=dim, tiled=True)  237 us
    all_to_all x1, blocking collectives, from_everyone(): lax.all_to_all(jnp.broadcast_to(value[None], (peers, *value.shape)), axis...  26.5 us
    dot_general x1, matrix products, body(): jnp.dot(hidden, down_weight, preferred_element_type=jnp.float32)  11.6 us
    unnamed x1, blocking collectives  6.78 us
  transfers between devices with their start and end apart: 3, of which 3 were waited for; matrix products, arithmetic and copies ran while one was open for 0% of the time, Pallas kernels for 0%

commit v1 on v0

v1 whole, which is shorter than its diff:
```python
import functools

import jax
import jax.numpy as jnp
from jax import lax
from jax.experimental import pallas as pl
from jax.experimental.pallas import tpu as pltpu
from jax.sharding import Mesh
from jax.sharding import PartitionSpec as P

F32 = jnp.float32
BF16 = jnp.bfloat16
D = 16384
N = 4096
K = 832
KP = 896
TILE = 512
WIDTHS = (2048, 2048)
STARTS = (0, 2048)
COLOURS = ("x", "y")
LAST = F32


def kernel(
    gate_hbm, up_hbm, w_hbm, res_ref, gain_ref, stream_ref, normed_ref,
    gate_v, up_v, w_v, h,
    p32_x, p16_x, p32_y, p16_y,
    ra_x, rb_x, rc_x, c_x, ra_y, rb_y, rc_y, c_y,
    q32_x, q16_x, q32_y, q16_y,
    r2_x, c2_x, r2_y, c2_y,
    t32_x, t16_x, t32_y, t16_y,
    r3_x, c3_x, r3_y, c3_y,
    sq_own, sq_in,
    in_sem, w_sem, ag_send, ag_recv, s1_send, s1_recv, s2_send, s2_recv, s3_send, s3_recv, n_send, n_recv,
):
    x, y, hi, lo, core = (lax.axis_index(a) for a in ("x", "y", "h", "l", "c"))

    def ring(axis, index, step):
        return {axis: lax.rem(index + step, 4)}

    sibling = {"c": 1 - core}
    across = {"l": 1 - lo}
    diagonal = {"l": 1 - lo, "c": 1 - core}
    partners = [sibling, across, diagonal]
    for axis, index in (("x", x), ("y", y), ("h", hi)):
        partners += [ring(axis, index, 1), ring(axis, index, 3)]

    barrier = pltpu.get_barrier_semaphore()
    for who in partners:
        pl.semaphore_signal(barrier, inc=1, device_id=who, device_id_type=pl.DeviceIdType.MESH)

    get_gate = pltpu.make_async_copy(gate_hbm, gate_v, in_sem.at[0])
    get_up = pltpu.make_async_copy(up_hbm, up_v, in_sem.at[1])
    get_gate.start()
    get_up.start()

    def get_w(j):
        cols = pl.ds(pl.multiple_of(j * TILE, TILE), TILE)
        return pltpu.make_async_copy(w_hbm.at[:, cols], w_v.at[pl.ds(0, K), cols], w_sem.at[j])

    for j in range(N // TILE):
        get_w(j).start()
    w_v[K:, :] = jnp.zeros((KP - K, N), BF16)
    get_gate.wait()
    get_up.wait()

    for k in range(KP // 128):
        depth = min(128, K - k * 128)
        g = gate_v[k * 128 : k * 128 + depth, :].astype(F32)
        u = up_v[k * 128 : k * 128 + depth, :].astype(F32)
        act = g / (1.0 + jnp.exp(-g)) * u
        if depth < 128:
            act = jnp.concatenate([act, jnp.zeros((128 - depth, 256), F32)], axis=0)
        h[0, :, k * 128 : (k + 1) * 128] = act.T.astype(BF16)

    pl.semaphore_wait(barrier, len(partners))

    def remote(src, dst, send, recv, who):
        return pltpu.make_async_remote_copy(
            src_ref=src, dst_ref=dst, send_sem=send, recv_sem=recv,
            device_id=who, device_id_type=pl.DeviceIdType.MESH,
        )

    gathers = [
        remote(h.at[0], h.at[1], ag_send.at[0], ag_recv.at[0], sibling),
        remote(h.at[0], h.at[2], ag_send.at[1], ag_recv.at[1], across),
        remote(h.at[2], h.at[3], ag_send.at[2], ag_recv.at[2], sibling),
    ]
    gathers[1].start()
    gathers[0].start()

    blocks = (2 * lo + core, 2 * lo + 1 - core, 2 * (1 - lo) + core, 2 * (1 - lo) + 1 - core)
    roles = [lax.rem(b + 4 - y, 4) for b in blocks]

    def rows(index, step, size):
        return pl.ds(pl.multiple_of(lax.rem(index + step, 4) * size, size), size)

    wx, wy = WIDTHS
    hx, hy = wx // 2, wy // 2

    def product(i, start, width, p32, p16, slot, first):
        def step(j, carry):
            if first:
                get_w(start // TILE + j).wait()
            cols = pl.ds(pl.multiple_of(j * TILE, TILE), TILE)
            from_cols = pl.ds(pl.multiple_of(start + j * TILE, TILE), TILE)
            part = jnp.dot(h[i], w_v[:, from_cols], preferred_element_type=F32)
            p32[slot, :, cols] = part
            p16[slot, :, cols] = part.astype(BF16)
            return carry

        lax.fori_loop(0, width // TILE, step, 0)

    def first_x(kind, i):
        sems = s1_send.at[0, kind, i], s1_recv.at[0, kind, i]
        low, high = pl.ds(0, hx), pl.ds(hx, hx)
        ahead, behind = ring("x", x, 1), ring("x", x, 3)
        return (
            lambda: remote(p16_x.at[i, rows(x, 2, 64), low], ra_x.at[0, i], *sems, ahead),
            lambda: remote(p16_x.at[i, rows(x, 2, 64), high], ra_x.at[1, i], *sems, behind),
            lambda: remote(p16_x.at[i, rows(x, 1, 64), high], rb_x.at[0, i], *sems, ahead),
            lambda: remote(p16_x.at[i, rows(x, 3, 64), low], rb_x.at[1, i], *sems, behind),
            lambda: remote(c_x.at[0, i], rc_x.at[0, i], *sems, ahead),
            lambda: remote(c_x.at[1, i], rc_x.at[1, i], *sems, behind),
        )[kind]()

    def first_y(kind, q):
        sems = s1_send.at[1, kind, q], s1_recv.at[1, kind, q]
        low, high = pl.ds(0, hy), pl.ds(hy, hy)
        ahead, behind = ring("y", y, 1), ring("y", y, 3)
        return (
            lambda: remote(p16_y.at[2, rows(x, q, 64), low], ra_y.at[0, q], *sems, ahead),
            lambda: remote(p16_y.at[2, rows(x, q, 64), high], ra_y.at[1, q], *sems, behind),
            lambda: remote(p16_y.at[1, rows(x, q, 64), high], rb_y.at[0, q], *sems, ahead),
            lambda: remote(p16_y.at[3, rows(x, q, 64), low], rb_y.at[1, q], *sems, behind),
            lambda: remote(c_y.at[0, q], rc_y.at[0, q], *sems, ahead),
            lambda: remote(c_y.at[1, q], rc_y.at[1, q], *sems, behind),
        )[kind]()

    order = (2, 1, 3, 0)

    def x_product(i, first=False):
        product(i, STARTS[0], wx, p32_x, p16_x, i, first)
        for kind in (0, 1, 2, 3):
            first_x(kind, i).start()

    def y_product(i, first=False):
        role = roles[i]
        product(i, STARTS[1], wy, p32_y, p16_y, role, first)
        for r, kinds in ((2, (0, 1)), (1, (2,)), (3, (3,))):

            @pl.when(role == r)
            def _():
                for q in order:
                    for kind in kinds:
                        first_y(kind, q).start()

    def x_relay(i):
        for s, step in ((0, 1), (1, 3)):
            first_x(s, i).wait_recv()
            mine = p32_x[i, rows(x, step, 64), s * hx : (s + 1) * hx]
            c_x[s, i] = (mine + ra_x[s, i].astype(F32)).astype(BF16)
            first_x(4 + s, i).start()

    def y_relay(s, q):
        first_y(s, q).wait_recv()
        mine = p32_y[1 + 2 * s, rows(x, q, 64), s * hy : (s + 1) * hy]
        c_y[s, q] = (mine + ra_y[s, q].astype(F32)).astype(BF16)
        first_y(4 + s, q).start()

    def y_relays(i):
        for s, r in ((0, 1), (1, 3)):

            @pl.when(roles[i] == r)
            def _():
                for q in order:
                    y_relay(s, q)

    def second(colour, kind):
        sems = s2_send.at[colour, kind], s2_recv.at[colour, kind]
        q16, r2, c2 = ((q16_x, r2_x, c2_x), (q16_y, r2_y, c2_y))[colour]
        half = (hx, hy)[colour]
        low, high = pl.ds(0, half), pl.ds(half, half)
        axis, index = (("y", y), ("x", x))[colour]
        ahead, behind = ring(axis, index, 1), ring(axis, index, 3)
        return (
            lambda: remote(q16.at[2, :, low], r2.at[0], *sems, ahead),
            lambda: remote(q16.at[2, :, high], r2.at[1], *sems, behind),
            lambda: remote(q16.at[1, :, high], r2.at[2], *sems, ahead),
            lambda: remote(q16.at[3, :, low], r2.at[3], *sems, behind),
            lambda: remote(c2.at[0], r2.at[4], *sems, ahead),
            lambda: remote(c2.at[1], r2.at[5], *sems, behind),
        )[kind]()

    def x_finish(i):
        for kind in (2, 3, 4, 5):
            first_x(kind, i).wait_recv()
        role = roles[i]
        low = p32_x[i, rows(x, 0, 64), :hx] + rc_x[0, i].astype(F32) + rb_x[1, i].astype(F32)
        q32_x[role, :, :hx] = low
        q16_x[role, :, :hx] = low.astype(BF16)
        high = p32_x[i, rows(x, 0, 64), hx:] + rb_x[0, i].astype(F32) + rc_x[1, i].astype(F32)
        q32_x[role, :, hx:] = high
        q16_x[role, :, hx:] = high.astype(BF16)
        for r, kinds in ((2, (0, 1)), (1, (2,)), (3, (3,))):

            @pl.when(role == r)
            def _():
                for kind in kinds:
                    second(0, kind).start()

    def y_finish(q):
        for kind in (2, 3, 4, 5):
            first_y(kind, q).wait_recv()
        low = p32_y[0, rows(x, q, 64), :hy] + rc_y[0, q].astype(F32) + rb_y[1, q].astype(F32)
        q32_y[q, :, :hy] = low
        q16_y[q, :, :hy] = low.astype(BF16)
        high = p32_y[0, rows(x, q, 64), hy:] + rb_y[0, q].astype(F32) + rc_y[1, q].astype(F32)
        q32_y[q, :, hy:] = high
        q16_y[q, :, hy:] = high.astype(BF16)
        for kind in {2: (0, 1), 1: (2,), 3: (3,), 0: ()}[q]:
            second(1, kind).start()

    def second_relay(colour, s):
        q32, r2, c2 = ((q32_x, r2_x, c2_x), (q32_y, r2_y, c2_y))[colour]
        half = (hx, hy)[colour]
        second(colour, s).wait_recv()
        mine = q32[1 + 2 * s, :, s * half : (s + 1) * half]
        c2[s] = (mine + r2[s].astype(F32)).astype(BF16)
        second(colour, 4 + s).start()

    def third(colour, kind):
        sems = s3_send.at[colour, kind], s3_recv.at[colour, kind]
        t16, r3, c3 = ((t16_x, r3_x, c3_x), (t16_y, r3_y, c3_y))[colour]
        half = (hx, hy)[colour]
        low, high = pl.ds(0, half), pl.ds(half, half)
        ahead, behind = ring("h", hi, 1), ring("h", hi, 3)
        return (
            lambda: remote(t16.at[rows(hi, 2, 16), low], r3.at[0], *sems, ahead),
            lambda: remote(t16.at[rows(hi, 2, 16), high], r3.at[1], *sems, behind),
            lambda: remote(t16.at[rows(hi, 1, 16), high], r3.at[2], *sems, ahead),
            lambda: remote(t16.at[rows(hi, 3, 16), low], r3.at[3], *sems, behind),
            lambda: remote(c3.at[0], r3.at[4], *sems, ahead),
            lambda: remote(c3.at[1], r3.at[5], *sems, behind),
        )[kind]()

    def second_finish(colour):
        q32, r2, t32, t16 = ((q32_x, r2_x, t32_x, t16_x), (q32_y, r2_y, t32_y, t16_y))[colour]
        half = (hx, hy)[colour]
        for kind in (2, 3, 4, 5):
            second(colour, kind).wait_recv()
        low = q32[0, :, :half] + r2[4].astype(F32) + r2[3].astype(F32)
        t32[:, :half] = low
        t16[:, :half] = low.astype(LAST)
        high = q32[0, :, half:] + r2[2].astype(F32) + r2[5].astype(F32)
        t32[:, half:] = high
        t16[:, half:] = high.astype(LAST)
        for kind in (0, 1, 2, 3):
            third(colour, kind).start()

    def third_relay(colour, s):
        t32, r3, c3 = ((t32_x, r3_x, c3_x), (t32_y, r3_y, c3_y))[colour]
        half = (hx, hy)[colour]
        third(colour, s).wait_recv()
        mine = t32[rows(hi, 1 + 2 * s, 16), s * half : (s + 1) * half]
        c3[s] = (mine + r3[s].astype(F32)).astype(LAST)
        third(colour, 4 + s).start()

    def third_finish(colour):
        t32, r3 = ((t32_x, r3_x), (t32_y, r3_y))[colour]
        half, start = (hx, hy)[colour], STARTS[colour]
        for kind in (2, 3, 4, 5):
            third(colour, kind).wait_recv()
        squares = jnp.zeros((16, 128), F32)
        for s, (a, b) in ((0, (4, 3)), (1, (2, 5))):
            for j in range(half // 128):
                here = s * half + j * 128
                cols = pl.ds(j * 128, 128)
                summed = t32[rows(hi, 0, 16), pl.ds(here, 128)] + r3[a, :, cols].astype(F32) + r3[b, :, cols].astype(F32)
                summed = summed + res_ref[:, pl.ds(start + here, 128)].astype(F32)
                t32[rows(hi, 0, 16), pl.ds(here, 128)] = summed
                stream_ref[:, pl.ds(start + here, 128)] = summed.astype(BF16)
                squares = squares + summed * summed
        return squares

    x_product(0, first=True)
    gathers[0].wait_recv()
    x_product(1)
    y_product(0, first=True)
    y_product(1)
    x_relay(0)
    gathers[1].wait_recv()
    gathers[2].start()
    x_product(2)
    y_product(2)
    gathers[2].wait_recv()
    x_product(3)
    y_product(3)
    x_relay(1)
    y_relays(0)
    y_relays(1)
    x_relay(2)
    y_relays(2)
    x_finish(0)
    x_relay(3)
    y_relays(3)
    x_finish(1)
    x_finish(2)
    x_finish(3)
    second_relay(0, 0)
    second_relay(0, 1)
    for q in order:
        y_finish(q)
    second_finish(0)
    second_relay(1, 0)
    second_relay(1, 1)
    third_relay(0, 0)
    third_relay(0, 1)
    second_finish(1)
    total = third_finish(0)
    third_relay(1, 0)
    third_relay(1, 1)
    total = total + third_finish(1)

    sq_own[...] = total
    exchange = [
        remote(sq_own, sq_in.at[i], n_send.at[i], n_recv.at[i], who)
        for i, who in enumerate((sibling, across, diagonal))
    ]
    for copy in exchange:
        copy.start()
    for copy in exchange:
        copy.wait_recv()
    for i in range(3):
        total = total + sq_in[i]
    scale = lax.rsqrt(jnp.sum(total, axis=1, keepdims=True) / D + 1e-05)
    for colour, t32 in enumerate((t32_x, t32_y)):
        for j in range(WIDTHS[colour] // 128):
            at = STARTS[colour] + j * 128
            gain = gain_ref[at // 128 : at // 128 + 1, :].astype(F32)
            scaled = t32[rows(hi, 0, 16), pl.ds(j * 128, 128)] * scale * gain
            normed_ref[:, pl.ds(at, 128)] = scaled.astype(BF16)

    for copy in gathers + exchange:
        copy.wait_send()
    for kind in range(6):
        for piece in range(4):
            first_x(kind, piece).wait_send()
            first_y(kind, piece).wait_send()
        for colour in range(2):
            second(colour, kind).wait_send()
            third(colour, kind).wait_send()


def body(gate_in, up_in, down_weight, residual, norm_gain):
    dma = pltpu.SemaphoreType.DMA
    scratch = [
        pltpu.VMEM((K, 256), BF16),
        pltpu.VMEM((K, 256), BF16),
        pltpu.VMEM((KP, N), BF16),
        pltpu.VMEM((4, 256, KP), BF16),
    ]
    for width in WIDTHS:
        scratch += [pltpu.VMEM((4, 256, width), F32), pltpu.VMEM((4, 256, width), BF16)]
    for width in WIDTHS:
        scratch += [pltpu.VMEM((2, 4, 64, width // 2), BF16)] * 4
    for width in WIDTHS:
        scratch += [pltpu.VMEM((4, 64, width), F32), pltpu.VMEM((4, 64, width), BF16)]
    for width in WIDTHS:
        scratch += [pltpu.VMEM((6, 64, width // 2), BF16), pltpu.VMEM((2, 64, width // 2), BF16)]
    for width in WIDTHS:
        scratch += [pltpu.VMEM((64, width), F32), pltpu.VMEM((64, width), LAST)]
    for width in WIDTHS:
        scratch += [pltpu.VMEM((6, 16, width // 2), LAST), pltpu.VMEM((2, 16, width // 2), LAST)]
    scratch += [
        pltpu.VMEM((16, 128), F32),
        pltpu.VMEM((3, 16, 128), F32),
        dma((2,)),
        dma((N // TILE,)),
        dma((3,)),
        dma((3,)),
        dma((2, 6, 4)),
        dma((2, 6, 4)),
        dma((2, 6)),
        dma((2, 6)),
        dma((2, 6)),
        dma((2, 6)),
        dma((3,)),
        dma((3,)),
    ]
    anywhere = pl.BlockSpec(memory_space=pl.ANY)
    vmem = pl.BlockSpec(memory_space=pltpu.VMEM)
    out = jax.ShapeDtypeStruct((16, N), BF16)
    return pl.pallas_call(
        kernel,
        out_shape=(out, out),
        in_specs=[anywhere, anywhere, anywhere, vmem, vmem],
        out_specs=(vmem, vmem),
        scratch_shapes=scratch,
        compiler_params=pltpu.CompilerParams(
            collective_id=0, has_side_effects=True, vmem_limit_bytes=60 * 1024 * 1024
        ),
    )(gate_in.T, up_in.T, down_weight, residual, norm_gain.reshape(N // 128, 128))


def solution(mesh):
    split = Mesh(mesh.devices.reshape(4, 4, 4, 2, 2), ("y", "x", "h", "l", "c"))
    tp, col = ("y", "x", "h"), ("l", "c")
    return jax.shard_map(
        body,
        mesh=split,
        in_specs=(P(col, tp), P(col, tp), P(tp, col), P(tp, col), P(col)),
        out_specs=(P(tp, col), P(tp, col)),
        check_vma=False,
    )
```

time: 303 us -> 97.4 us (0.32)
  waiting for transfers between devices: 237 us -> 0 us
  Pallas kernels: 0 us -> 93.1 us
  blocking collectives: 33.2 us -> 0 us
  between operations: 14.5 us -> 0.64 us
  matrix products: 11.6 us -> 0 us
  other arithmetic: 4.24 us -> 0 us
    reduce_scatter x3 -> x0, waiting for transfers between devices: 237 us -> none  [summed_rows(): nearer = lax.psum_scatter(value, axes[0], scatter_dimension=dim, tiled=True)]
    pallas_call x0 -> x1, Pallas kernels: none -> 93.1 us  [body(): pl.pallas_call(kernel, out_shape=(out, out), in_specs=[anywhere, anywhere...]
    all_to_all x1 -> x0, blocking collectives: 26.5 us -> none  [from_everyone(): lax.all_to_all(jnp.broadcast_to(value[None], (peers, *value.shape)), axis...]
    dot_general x1 -> x0, matrix products: 11.6 us -> none  [body(): jnp.dot(hidden, down_weight, preferred_element_type=jnp.float32)]
    unnamed x1 -> x0, blocking collectives: 6.78 us -> none
    convert_element_type x3 -> x0, other arithmetic: 3.12 us -> none  [the longest x1 1.7 us: body(): return (summed.astype(jnp.bfloat16), scaled.astype(jnp.bfloat16))]
  transfers between devices with their start and end apart: 3 -> 0, of which waited for: 3 -> 0; matrix products, arithmetic and copies ran while one was open for 0% -> 0% of each run, Pallas kernels for 0% -> 0%
where the time goes in v1:
time: 97.4 us; the launch traced here: 96.9 us
  Pallas kernels  93.1 us (96%)
  local copies, waits for them, and re-layouts  3.14 us (3%)
    pallas_call x1, Pallas kernels, body(): pl.pallas_call(kernel, out_shape=(out, out), in_specs=[anywhere, anywhere...  93.1 us
    unnamed x2, local copies, waits for them, and re-layouts  3.14 us

profile of v1, /device:TPU:1, one launch (start us, length us, event | category | flops | bytes accessed | tf_op | source)
XLA Modules:
  0.0 96.9 jit_solution(10002298969466036900)
XLA Ops:
  0.6 93.1 %shard_map.68 = (bf16[16,4096]{1,0:T(8,128)(2,1)}, bf16[16,4096]{1,0:T(8,128)(2,1)}) custom-call(bf16[832,256]{1,0:T(8,128)(2,1)} %bitcast.3, bf16[832,256]{1,0:T(8,128)(2,1)} %bitcast.4, bf16[832,4096]{1,0:T(8,128)(2,1)} %w_hbm.1, bf16[16,4096]{1,0:T(8,128)(2,1)} %res_ref.1, bf16[32,128]{1,0:T(8,128)(2,1)} %bitcast.5), custom_call_target="tpu_custom_call" | custom-call | tf_op jit(solution)/shard_map/pallas_call | solution.py:394
  93.8 1.6 %copy.9 = bf16[16,4096]{1,0:T(8,128)(2,1)} copy(bf16[16,4096]{1,0:T(8,128)(2,1)} %get-tuple-element.4) | data formatting | bytes 262144
  95.4 1.6 %copy.10 = bf16[16,4096]{1,0:T(8,128)(2,1)} copy(bf16[16,4096]{1,0:T(8,128)(2,1)} %get-tuple-element.5) | data formatting | bytes 262144

commit v2 on v0

v2 whole, which is shorter than its diff:
```python
import functools

import jax
import jax.numpy as jnp
from jax import lax
from jax.experimental import pallas as pl
from jax.experimental.pallas import tpu as pltpu
from jax.sharding import Mesh
from jax.sharding import PartitionSpec as P

F32 = jnp.float32
BF16 = jnp.bfloat16
D = 16384
N = 4096
K = 832
KP = 896
TILE = 512
VMEM_LIMIT = 58 * 1024 * 1024
WX = 2048
WY = N - WX
HX, QY = WX // 2, WY // 4
HY = QY // 2
LAST_X = BF16
LAST_Y = F32


def kernel(
    gate_hbm, up_hbm, w_hbm, res_ref, gain_ref, out_ref,
    gate_v, up_v, w_v, h,
    p32_x, p16_x, p32_y, p16_y,
    ra_x, rb_x, rc_x, c_x, ra_y, rb_y, rc_y, c_y,
    r2_x, c2_x, r2_y, c2_y,
    t32_x, t16_x, t32_y, t16_y,
    r3_x, c3_x, r3_y, c3_y,
    u_y, turned, summed, sq_own, sq_in,
    in_sem, w_sem, ag_send, ag_recv, s1_send, s1_recv, sx2_send, sx2_recv, sy2_send, sy2_recv,
    sx3_send, sx3_recv, sy3_send, sy3_recv, turn_send, turn_recv, n_send, n_recv,
):
    x, y, hi, lo, core = (lax.axis_index(a) for a in ("x", "y", "h", "l", "c"))
    scope = jax.named_scope

    def ring(axis, index, step):
        return {axis: lax.rem(index + step, 4)}

    get_gate = pltpu.make_async_copy(gate_hbm, gate_v, in_sem.at[0])
    get_up = pltpu.make_async_copy(up_hbm, up_v, in_sem.at[1])
    get_gate.start()
    get_up.start()

    def get_w(j):
        cols = pl.ds(pl.multiple_of(j * TILE, TILE), TILE)
        return pltpu.make_async_copy(w_hbm.at[:, cols], w_v.at[pl.ds(0, K), cols], w_sem.at[j])

    sibling = {"c": 1 - core}
    across = {"l": 1 - lo}
    diagonal = {"l": 1 - lo, "c": 1 - core}
    partners = [sibling, across, diagonal, ring("y", y, 2)]
    for axis, index in (("x", x), ("y", y), ("h", hi)):
        partners += [ring(axis, index, 1), ring(axis, index, 3)]

    barrier = pltpu.get_barrier_semaphore()
    for who in partners:
        pl.semaphore_signal(barrier, inc=1, device_id=who, device_id_type=pl.DeviceIdType.MESH)

    for j in range(HX // TILE):
        get_w(j).start()
    w_v[K:, :] = jnp.zeros((KP - K, N), BF16)
    with scope("get_in"):
        get_gate.wait()
        get_up.wait()
    for j in range(HX // TILE, N // TILE):
        get_w(j).start()

    for k in range(KP // 128):
        depth = min(128, K - k * 128)
        g = gate_v[k * 128 : k * 128 + depth, :].astype(F32)
        u = up_v[k * 128 : k * 128 + depth, :].astype(F32)
        act = g / (1.0 + jnp.exp(-g)) * u
        if depth < 128:
            act = jnp.concatenate([act, jnp.zeros((128 - depth, 256), F32)], axis=0)
        h[0, :, k * 128 : (k + 1) * 128] = act.T.astype(BF16)

    with scope("barrier"):
        pl.semaphore_wait(barrier, len(partners))

    def remote(src, dst, send, recv, who):
        return pltpu.make_async_remote_copy(
            src_ref=src, dst_ref=dst, send_sem=send, recv_sem=recv,
            device_id=who, device_id_type=pl.DeviceIdType.MESH,
        )

    gathers = [
        remote(h.at[0], h.at[1], ag_send.at[0], ag_recv.at[0], sibling),
        remote(h.at[0], h.at[2], ag_send.at[1], ag_recv.at[1], across),
        remote(h.at[2], h.at[3], ag_send.at[2], ag_recv.at[2], sibling),
    ]
    gathers[1].start()
    gathers[0].start()

    blocks = (2 * lo + core, 2 * lo + 1 - core, 2 * (1 - lo) + core, 2 * (1 - lo) + 1 - core)
    roles = [lax.rem(b + 4 - y, 4) for b in blocks]

    def rows(index, step, size):
        return pl.ds(pl.multiple_of(lax.rem(index + step, 4) * size, size), size)

    low_x, high_x = pl.ds(0, HX), pl.ds(HX, HX)
    low_y, high_y = pl.ds(0, HY), pl.ds(HY, HY)
    x_ways, y_ways, h_ways = (
        (ring(a, index, 1), ring(a, index, 3)) for a, index in (("x", x), ("y", y), ("h", hi))
    )

    def message(kind, sources, targets, send, recv, ways):
        return remote(sources[kind](), targets[kind](), send, recv, ways[kind % 2])

    def x1(kind, i):
        return message(
            kind,
            (
                lambda: p16_x.at[i, rows(x, 2, 64), low_x],
                lambda: p16_x.at[i, rows(x, 2, 64), high_x],
                lambda: p16_x.at[i, rows(x, 1, 64), high_x],
                lambda: p16_x.at[i, rows(x, 3, 64), low_x],
                lambda: c_x.at[0, i],
                lambda: c_x.at[1, i],
            ),
            [lambda k=k: (ra_x, rb_x, rc_x)[k // 2].at[k % 2, i] for k in range(6)],
            s1_send.at[0, kind, i], s1_recv.at[0, kind, i], x_ways,
        )

    def y1(kind, i):
        return message(
            kind,
            (
                lambda: p16_y.at[i, 2, :, :, :, low_y],
                lambda: p16_y.at[i, 2, :, :, :, high_y],
                lambda: p16_y.at[i, 1, :, :, :, high_y],
                lambda: p16_y.at[i, 3, :, :, :, low_y],
                lambda: c_y.at[0, i],
                lambda: c_y.at[1, i],
            ),
            [lambda k=k: (ra_y, rb_y, rc_y)[k // 2].at[k % 2, i] for k in range(6)],
            s1_send.at[1, kind, i], s1_recv.at[1, kind, i], y_ways,
        )

    def x2(kind, i):
        mine = rows(x, 0, 64)
        return message(
            kind,
            (
                lambda: p16_x.at[i, mine, low_x],
                lambda: p16_x.at[i, mine, high_x],
                lambda: p16_x.at[i, mine, high_x],
                lambda: p16_x.at[i, mine, low_x],
                lambda: c2_x.at[0],
                lambda: c2_x.at[1],
            ),
            [lambda k=k: r2_x.at[k] for k in range(6)],
            sx2_send.at[kind], sx2_recv.at[kind], y_ways,
        )

    def y2(kind, i):
        return message(
            kind,
            (
                lambda: p16_y.at[i, 0, :, lax.rem(hi + 2, 4), :, low_y],
                lambda: p16_y.at[i, 0, :, lax.rem(hi + 2, 4), :, high_y],
                lambda: p16_y.at[i, 0, :, lax.rem(hi + 1, 4), :, high_y],
                lambda: p16_y.at[i, 0, :, lax.rem(hi + 3, 4), :, low_y],
                lambda: c2_y.at[0, i],
                lambda: c2_y.at[1, i],
            ),
            [lambda k=k: r2_y.at[k, i] for k in range(6)],
            sy2_send.at[kind, i], sy2_recv.at[kind, i], h_ways,
        )

    def x3(kind):
        return message(
            kind,
            (
                lambda: t16_x.at[rows(hi, 2, 16), low_x],
                lambda: t16_x.at[rows(hi, 2, 16), high_x],
                lambda: t16_x.at[rows(hi, 1, 16), high_x],
                lambda: t16_x.at[rows(hi, 3, 16), low_x],
                lambda: c3_x.at[0],
                lambda: c3_x.at[1],
            ),
            [lambda k=k: r3_x.at[k] for k in range(6)],
            sx3_send.at[kind], sx3_recv.at[kind], h_ways,
        )

    def y3(kind, g):
        pair = pl.ds(2 * g, 2)
        return message(
            kind,
            (
                lambda: t16_y.at[pair, lax.rem(x + 2, 4), :, low_y],
                lambda: t16_y.at[pair, lax.rem(x + 2, 4), :, high_y],
                lambda: t16_y.at[pair, lax.rem(x + 1, 4), :, high_y],
                lambda: t16_y.at[pair, lax.rem(x + 3, 4), :, low_y],
                lambda: c3_y.at[0, g],
                lambda: c3_y.at[1, g],
            ),
            [lambda k=k: r3_y.at[k, g] for k in range(6)],
            sy3_send.at[kind, g], sy3_recv.at[kind, g], x_ways,
        )

    def x_product(i, first=False):
        with scope(f"x_product{i}"):
            for half in range(2):

                def step(j, carry):
                    j = half * (HX // TILE) + j
                    if first:
                        get_w(j).wait()
                    cols = pl.ds(pl.multiple_of(j * TILE, TILE), TILE)
                    part = jnp.dot(h[i], w_v[:, cols], preferred_element_type=F32)
                    p32_x[i, :, cols] = part
                    p16_x[i, :, cols] = part.astype(BF16)
                    return carry

                lax.fori_loop(0, HX // TILE, step, 0)
                for kind in ((0, 3), (1, 2))[half]:
                    x1(kind, i).start()

    def y_product(i, first=False):
        with scope(f"y_product{i}"):

            def quarter(r):
                at = lax.rem(y + r, 4)
                if first:
                    get_w(WX // TILE + at).wait()
                cols = pl.ds(pl.multiple_of(WX + at * QY, QY), QY)
                part = jnp.dot(h[i], w_v[:, cols], preferred_element_type=F32).reshape(4, 4, 16, QY)
                p32_y[i, r] = part
                p16_y[i, r] = part.astype(BF16)

            quarter(2)
            for kind in (0, 1):
                y1(kind, i).start()
            lax.fori_loop(0, 3, lambda j, c: (quarter(lax.rem(5 - j, 4)), c)[1], 0)
            for kind in (2, 3):
                y1(kind, i).start()

    def x_relay(i):
        with scope(f"x_relay{i}"):
            for s, step in ((0, 1), (1, 3)):
                x1(s, i).wait_recv()
                mine = p32_x[i, rows(x, step, 64), s * HX : (s + 1) * HX]
                c_x[s, i] = (mine + ra_x[s, i].astype(F32)).astype(BF16)
                x1(4 + s, i).start()

    def y_relay(i):
        with scope(f"y_relay{i}"):
            for s, r in ((0, 1), (1, 3)):
                y1(s, i).wait_recv()
                mine = p32_y[i, r, :, :, :, s * HY : (s + 1) * HY]
                c_y[s, i] = (mine + ra_y[s, i].astype(F32)).astype(BF16)
                y1(4 + s, i).start()

    def x_finish(i):
        with scope(f"x_finish{i}"):
            for kind in (2, 3, 4, 5):
                x1(kind, i).wait_recv()
            mine = rows(x, 0, 64)
            for s, (a, b) in ((0, (rc_x[0, i], rb_x[1, i])), (1, (rb_x[0, i], rc_x[1, i]))):
                cols = pl.ds(s * HX, HX)
                total = p32_x[i, mine, cols] + a.astype(F32) + b.astype(F32)
                p32_x[i, mine, cols] = total
                p16_x[i, mine, cols] = total.astype(BF16)
            for r, kinds in ((2, (0, 1)), (1, (2,)), (3, (3,))):

                @pl.when(roles[i] == r)
                def _():
                    for kind in kinds:
                        x2(kind, i).start()

    def y_finish(i):
        with scope(f"y_finish{i}"):
            for kind in (2, 3, 4, 5):
                y1(kind, i).wait_recv()
            for s, (a, b) in ((0, (rc_y[0, i], rb_y[1, i])), (1, (rb_y[0, i], rc_y[1, i]))):
                cols = pl.ds(s * HY, HY)
                total = p32_y[i, 0, :, :, :, cols] + a.astype(F32) + b.astype(F32)
                p32_y[i, 0, :, :, :, cols] = total
                p16_y[i, 0, :, :, :, cols] = total.astype(BF16)
            for kind in (0, 1, 2, 3):
                y2(kind, i).start()

    def x_relay2(i):
        with scope(f"x_second{i}"):
            for s, r in ((0, 1), (1, 3)):

                @pl.when(roles[i] == r)
                def _():
                    x2(s, i).wait_recv()
                    mine = p32_x[i, rows(x, 0, 64), s * HX : (s + 1) * HX]
                    c2_x[s] = (mine + r2_x[s].astype(F32)).astype(BF16)
                    x2(4 + s, i).start()

    def y_relay2(i):
        with scope(f"y_second{i}"):
            for s, step in ((0, 1), (1, 3)):
                y2(s, i).wait_recv()
                mine = p32_y[i, 0, :, lax.rem(hi + step, 4), :, s * HY : (s + 1) * HY]
                c2_y[s, i] = (mine + r2_y[s, i].astype(F32)).astype(BF16)
                y2(4 + s, i).start()

    def x_finish2(i):
        with scope("x_finish_second"):
            for kind in (2, 3, 4, 5):
                x2(kind, i).wait_recv()
            for s, (a, b) in ((0, (4, 3)), (1, (2, 5))):
                cols = pl.ds(s * HX, HX)
                total = p32_x[i, rows(x, 0, 64), cols] + r2_x[a].astype(F32) + r2_x[b].astype(F32)
                t32_x[:, cols] = total
                t16_x[:, cols] = total.astype(LAST_X)
            for kind in (0, 1, 2, 3):
                x3(kind).start()

    def y_finish2(g):
        with scope(f"y_finish_second{g}"):
            for i in (2 * g, 2 * g + 1):
                for kind in (2, 3, 4, 5):
                    y2(kind, i).wait_recv()
                for s, (a, b) in ((0, (4, 3)), (1, (2, 5))):
                    cols = pl.ds(s * HY, HY)
                    total = p32_y[i, 0, :, hi, :, cols] + r2_y[a, i].astype(F32) + r2_y[b, i].astype(F32)
                    t32_y[i, :, :, cols] = total
                    t16_y[i, :, :, cols] = total.astype(LAST_Y)
            for kind in (0, 1, 2, 3):
                y3(kind, g).start()

    def x_relay3():
        with scope("x_third"):
            for s in range(2):
                x3(s).wait_recv()
                mine = t32_x[rows(hi, 1 + 2 * s, 16), s * HX : (s + 1) * HX]
                c3_x[s] = (mine + r3_x[s].astype(F32)).astype(LAST_X)
                x3(4 + s).start()

    def y_relay3(g):
        with scope(f"y_third{g}"):
            for s in range(2):
                y3(s, g).wait_recv()
                mine = t32_y[2 * g : 2 * g + 2, lax.rem(x + 1 + 2 * s, 4), :, s * HY : (s + 1) * HY]
                c3_y[s, g] = (mine + r3_y[s, g].astype(F32)).astype(LAST_Y)
                y3(4 + s, g).start()

    def turn(i):
        d = lax.rem(y + 4 - blocks[i], 4)
        return remote(u_y.at[i], turned.at[d], turn_send.at[i], turn_recv.at[d], {"y": blocks[i]})

    def y_finish3(g):
        with scope(f"y_finish_third{g}"):
            for kind in (2, 3, 4, 5):
                y3(kind, g).wait_recv()
            for i in (2 * g, 2 * g + 1):
                for s, (a, b) in ((0, (4, 3)), (1, (2, 5))):
                    cols = pl.ds(s * HY, HY)
                    total = t32_y[i, x, :, cols]
                    total = total + r3_y[a, g, i % 2].astype(F32) + r3_y[b, g, i % 2].astype(F32)
                    u_y[i, :, cols] = total

                @pl.when(roles[i] != 0)
                def _():
                    turn(i).start()

    def folded(value):
        total = value[:, :128]
        for j in range(1, value.shape[1] // 128):
            total = total + value[:, j * 128 : (j + 1) * 128]
        return total

    def x_finish3():
        with scope("x_finish_third"):
            for kind in (2, 3, 4, 5):
                x3(kind).wait_recv()
            squares = jnp.zeros((16, 128), F32)
            for s, (a, b) in ((0, (4, 3)), (1, (2, 5))):
                cols = pl.ds(s * HX, HX)
                total = t32_x[rows(hi, 0, 16), cols] + r3_x[a].astype(F32) + r3_x[b].astype(F32)
                total = total + res_ref[:, cols].astype(F32)
                summed[:, cols] = total
                out_ref[0, :, cols] = total.astype(BF16)
                squares = squares + folded(total * total)
            return squares

    def y_close(squares):
        with scope("y_close"):
            own = 2 * lax.rem(y // 2 + lo, 2) + lax.rem(y + core, 2)
            for d in range(4):
                if d:
                    turn_in = remote(
                        turned.at[d], turned.at[d], turn_send.at[0], turn_recv.at[d], {"y": lax.rem(y + d, 4)}
                    )
                    turn_in.wait_recv()
                value = turned[d] if d else u_y[own]
                cols = pl.ds(pl.multiple_of(WX + lax.rem(y + d, 4) * QY, QY), QY)
                total = value + res_ref[:, cols].astype(F32)
                summed[:, cols] = total
                out_ref[0, :, cols] = total.astype(BF16)
                squares = squares + folded(total * total)
            return squares

    x_product(0, first=True)
    y_product(0, first=True)
    with scope("gather0"):
        gathers[0].wait_recv()
    x_product(1)
    y_product(1)
    x_relay(0)
    y_relay(0)
    with scope("gather1"):
        gathers[1].wait_recv()
    gathers[2].start()
    y_product(2)
    x_product(2)
    x_relay(1)
    y_relay(1)
    with scope("gather2"):
        gathers[2].wait_recv()
    y_product(3)
    x_product(3)
    y_finish(0)
    x_finish(0)
    y_relay(2)
    x_relay(2)
    y_finish(1)
    x_finish(1)
    y_relay2(0)
    x_relay2(0)
    y_relay(3)
    x_relay(3)
    y_relay2(1)
    x_relay2(1)
    y_finish2(0)
    y_finish(2)
    x_finish(2)
    y_finish(3)
    x_finish(3)
    y_relay3(0)
    y_relay2(2)
    x_relay2(2)
    y_relay2(3)
    x_relay2(3)
    y_finish3(0)
    own_slot = 2 * lax.rem(y // 2 + lo, 2) + lax.rem(y + core, 2)
    y_finish2(1)
    x_finish2(own_slot)
    y_relay3(1)
    x_relay3()
    y_finish3(1)
    total = y_close(x_finish3())

    sq_own[...] = total
    exchange = [
        remote(sq_own, sq_in.at[i], n_send.at[i], n_recv.at[i], who)
        for i, who in enumerate((sibling, across, diagonal))
    ]
    for copy in exchange:
        copy.start()
    with scope("drain"):
        for copy in gathers:
            copy.wait_send()
        for kind in range(6):
            for i in range(4):
                x1(kind, i).wait_send()
                y1(kind, i).wait_send()
                y2(kind, i).wait_send()
            x2(kind, 0).wait_send()
            x3(kind).wait_send()
            for g in range(2):
                y3(kind, g).wait_send()
        for i in range(4):

            @pl.when(roles[i] != 0)
            def _():
                turn(i).wait_send()

    with scope("exchange"):
        for copy in exchange:
            copy.wait_recv()
    for i in range(3):
        total = total + sq_in[i]
    scale = lax.rsqrt(jnp.sum(total, axis=1, keepdims=True) / D + 1e-05)
    for j in range(N // 128):
        cols = pl.ds(j * 128, 128)
        out_ref[1, :, cols] = (summed[:, cols] * scale * gain_ref[j : j + 1, :].astype(F32)).astype(BF16)
    for copy in exchange:
        copy.wait_send()


def body(gate_in, up_in, down_weight, residual, norm_gain):
    dma = pltpu.SemaphoreType.DMA
    vm = pltpu.VMEM
    scratch = [vm((K, 256), BF16), vm((K, 256), BF16), vm((KP, N), BF16), vm((4, 256, KP), BF16)]
    scratch += [vm((4, 256, WX), F32), vm((4, 256, WX), BF16)]
    scratch += [vm((4, 4, 4, 4, 16, QY), F32), vm((4, 4, 4, 4, 16, QY), BF16)]
    scratch += [vm((2, 4, 64, HX), BF16)] * 4 + [vm((2, 4, 4, 4, 16, HY), BF16)] * 4
    scratch += [vm((6, 64, HX), BF16), vm((2, 64, HX), BF16), vm((6, 4, 4, 16, HY), BF16), vm((2, 4, 4, 16, HY), BF16)]
    scratch += [vm((64, WX), F32), vm((64, WX), LAST_X), vm((4, 4, 16, QY), F32), vm((4, 4, 16, QY), LAST_Y)]
    scratch += [vm((6, 16, HX), LAST_X), vm((2, 16, HX), LAST_X)]
    scratch += [vm((6, 2, 2, 16, HY), LAST_Y), vm((2, 2, 2, 16, HY), LAST_Y)]
    scratch += [vm((4, 16, QY), F32), vm((4, 16, QY), F32), vm((16, N), F32), vm((16, 128), F32), vm((3, 16, 128), F32)]
    sems = [(2,), (N // TILE,), (3,), (3,), (2, 6, 4), (2, 6, 4), (6,), (6,), (6, 4), (6, 4)]
    sems += [(6,), (6,), (6, 2), (6, 2), (4,), (4,), (3,), (3,)]
    scratch += [dma(shape) for shape in sems]
    anywhere = pl.BlockSpec(memory_space=pl.ANY)
    vmem = pl.BlockSpec(memory_space=pltpu.VMEM)
    both = pl.pallas_call(
        kernel,
        out_shape=jax.ShapeDtypeStruct((2, 16, N), BF16),
        in_specs=[anywhere, anywhere, anywhere, vmem, vmem],
        out_specs=vmem,
        scratch_shapes=scratch,
        compiler_params=pltpu.CompilerParams(
            collective_id=0, has_side_effects=True, vmem_limit_bytes=VMEM_LIMIT
        ),
    )(gate_in.T, up_in.T, down_weight, residual, norm_gain.reshape(N // 128, 128))
    return both[0], both[1]


def solution(mesh):
    split = Mesh(mesh.devices.reshape(4, 4, 4, 2, 2), ("y", "x", "h", "l", "c"))
    tp, col = ("y", "x", "h"), ("l", "c")
    return jax.shard_map(
        body,
        mesh=split,
        in_specs=(P(col, tp), P(col, tp), P(tp, col), P(tp, col), P(col)),
        out_specs=(P(tp, col), P(tp, col)),
        check_vma=False,
    )
```

time: 303 us -> 82.5 us (0.27)
  waiting for transfers between devices: 237 us -> 0 us
  Pallas kernels: 0 us -> 80 us
  blocking collectives: 33.2 us -> 0 us
  between operations: 14.5 us -> 0.64 us
  matrix products: 11.6 us -> 0 us
  other arithmetic: 4.24 us -> 0 us
    reduce_scatter x3 -> x0, waiting for transfers between devices: 237 us -> none  [summed_rows(): nearer = lax.psum_scatter(value, axes[0], scatter_dimension=dim, tiled=True)]
    pallas_call x0 -> x1, Pallas kernels: none -> 80 us  [body(): pl.pallas_call(kernel, out_shape=jax.ShapeDtypeStruct((2, 16, N), BF16),...]
    all_to_all x1 -> x0, blocking collectives: 26.5 us -> none  [from_everyone(): lax.all_to_all(jnp.broadcast_to(value[None], (peers, *value.shape)), axis...]
    dot_general x1 -> x0, matrix products: 11.6 us -> none  [body(): jnp.dot(hidden, down_weight, preferred_element_type=jnp.float32)]
    unnamed x1 -> x0, blocking collectives: 6.78 us -> none
    convert_element_type x3 -> x0, other arithmetic: 3.12 us -> none  [the longest x1 1.7 us: body(): return (summed.astype(jnp.bfloat16), scaled.astype(jnp.bfloat16))]
  transfers between devices with their start and end apart: 3 -> 0, of which waited for: 3 -> 0; matrix products, arithmetic and copies ran while one was open for 0% -> 0% of each run, Pallas kernels for 0% -> 0%
where the time goes in v2:
time: 82.5 us; the launch traced here: 82.3 us
  Pallas kernels  80 us (97%)
  local copies, waits for them, and re-layouts  1.68 us (2%)
    pallas_call x1, Pallas kernels, body(): pl.pallas_call(kernel, out_shape=jax.ShapeDtypeStruct((2, 16, N), BF16),...  80 us
    squeeze x1, local copies, waits for them, and re-layouts, body(): return (both[0], both[1])  1.68 us

profile of v2, /device:TPU:1, one launch (start us, length us, event | category | flops | bytes accessed | tf_op | source)
XLA Modules:
  0.0 82.3 jit_solution(9498645781369761531)
XLA Ops:
  0.6 80.0 %shard_map.68 = bf16[2,16,4096]{2,1,0:T(8,128)(2,1)} custom-call(bf16[832,256]{1,0:T(8,128)(2,1)} %bitcast.7, bf16[832,256]{1,0:T(8,128)(2,1)} %bitcast.8, bf16[832,4096]{1,0:T(8,128)(2,1)} %w_hbm.1, bf16[16,4096]{1,0:T(8,128)(2,1)} %res_ref.1, bf16[32,128]{1,0:T(8,128)(2,1)} %bitcast.9), custom_call_target="tpu_custom_call" | custom-call | tf_op jit(solution)/shard_map/pallas_call | solution.py:510
  80.7 1.7 %slice_bitcast_fusion = (bf16[16,4096]{1,0:T(8,128)(2,1)}, bf16[16,4096]{1,0:T(8,128)(2,1)}) fusion(bf16[2,16,4096]{2,1,0:T(8,128)(2,1)} %shard_map.68), kind=kLoop, calls=%fused_computation | loop fusion | bytes 524288 | tf_op jit(solution)/shard_map/squeeze | solution.py:520

commit v3 on v0

v3 whole, which is shorter than its diff:
```python
import functools

import jax
import jax.numpy as jnp
from jax import lax
from jax.experimental import pallas as pl
from jax.experimental.pallas import tpu as pltpu
from jax.sharding import Mesh
from jax.sharding import PartitionSpec as P

F32 = jnp.float32
BF16 = jnp.bfloat16
D = 16384
N = 4096
K = 832
KP = 896
TILE = 512
VMEM_LIMIT = 58 * 1024 * 1024
WX = 2048
WY = N - WX
HX, QY = WX // 2, WY // 4
HY = QY // 2
LAST_X = BF16
LAST_Y = F32


def kernel(
    gate_hbm, up_hbm, w_hbm, res_hbm, gain_hbm, out_ref,
    gate_v, up_v, res_ref, gain_ref, w_v, h,
    p32_x, p16_x, p32_y, p16_y,
    a1_x, bc1_x, c1_x, a1_y, bc1_y, c1_y,
    a2_x, bc2_x, c2_x, a2_y, bc2_y, c2_y,
    t32_x, t16_x, t32_y, t16_y,
    line, plane,
    summed, sq_own, sq_in,
    in_sem, w_sem, ag_send, ag_recv, send_sem, a1_recv, bc1_recv, a2_recv, bc2_recv, last_recv, n_sem,
):
    x, y, hi, lo, core = (lax.axis_index(a) for a in ("x", "y", "h", "l", "c"))
    scope = jax.named_scope

    def ring(axis, index, step):
        return {axis: lax.rem(index + step, 4)}

    get_gate = pltpu.make_async_copy(gate_hbm, gate_v, in_sem.at[0])
    get_up = pltpu.make_async_copy(up_hbm, up_v, in_sem.at[1])
    get_gate.start()
    get_up.start()

    def get_w(j):
        cols = pl.ds(pl.multiple_of(j * TILE, TILE), TILE)
        return pltpu.make_async_copy(w_hbm.at[:, cols], w_v.at[pl.ds(0, K), cols], w_sem.at[j])

    sibling = {"c": 1 - core}
    across = {"l": 1 - lo}
    diagonal = {"l": 1 - lo, "c": 1 - core}
    partners = [sibling, across, diagonal]
    partners += [ring("h", hi, 1), ring("h", hi, 3)]
    partners += [ring("y", y, d) | ring("x", x, e) for d in range(4) for e in range(4) if d + e]

    barrier = pltpu.get_barrier_semaphore()
    for who in partners:
        pl.semaphore_signal(barrier, inc=1, device_id=who, device_id_type=pl.DeviceIdType.MESH)

    for j in range(HX // TILE):
        get_w(j).start()
    w_v[K:, :] = jnp.zeros((KP - K, N), BF16)
    with scope("get_in"):
        get_gate.wait()
        get_up.wait()
    for j in range(HX // TILE, N // TILE):
        get_w(j).start()
    get_rest = [
        pltpu.make_async_copy(res_hbm, res_ref, in_sem.at[2]),
        pltpu.make_async_copy(gain_hbm, gain_ref, in_sem.at[3]),
    ]
    for copy in get_rest:
        copy.start()

    for k in range(KP // 128):
        depth = min(128, K - k * 128)
        g = gate_v[k * 128 : k * 128 + depth, :].astype(F32)
        u = up_v[k * 128 : k * 128 + depth, :].astype(F32)
        act = g / (1.0 + jnp.exp(-g)) * u
        if depth < 128:
            act = jnp.concatenate([act, jnp.zeros((128 - depth, 256), F32)], axis=0)
        h[0, :, k * 128 : (k + 1) * 128] = act.T.astype(BF16)

    with scope("barrier"):
        pl.semaphore_wait(barrier, len(partners))

    def remote(src, dst, send, recv, who):
        return pltpu.make_async_remote_copy(
            src_ref=src, dst_ref=dst, send_sem=send, recv_sem=recv,
            device_id=who, device_id_type=pl.DeviceIdType.MESH,
        )

    gathers = [
        remote(h.at[0], h.at[1], ag_send, ag_recv.at[0], sibling),
        remote(h.at[0], h.at[2], ag_send, ag_recv.at[1], across),
        remote(h.at[2], h.at[3], ag_send, ag_recv.at[2], sibling),
    ]
    gathers[1].start()
    gathers[0].start()

    blocks = (2 * lo + core, 2 * lo + 1 - core, 2 * (1 - lo) + core, 2 * (1 - lo) + 1 - core)
    roles = [lax.rem(b + 4 - y, 4) for b in blocks]

    def rows(index, step, size):
        return pl.ds(pl.multiple_of(lax.rem(index + step, 4) * size, size), size)

    low_x, high_x = pl.ds(0, HX), pl.ds(HX, HX)
    low_y, high_y = pl.ds(0, HY), pl.ds(HY, HY)
    x_ways, y_ways, h_ways = (
        (ring(a, index, 1), ring(a, index, 3)) for a, index in (("x", x), ("y", y), ("h", hi))
    )

    def message(stage, colour, kind, i, source):
        a, bc, ways = buffers[stage][colour]
        a_recv, bc_recv = ((a1_recv, bc1_recv), (a2_recv, bc2_recv))[stage]
        if kind < 2:
            target, recv = a.at[kind, i], a_recv.at[colour, kind, i]
        else:
            target, recv = bc.at[i, kind - 2], bc_recv.at[colour, i]
        return remote(source, target, send_sem.at[stage, colour, kind // 4], recv, ways[kind % 2])

    buffers = (((a1_x, bc1_x, x_ways), (a1_y, bc1_y, y_ways)), ((a2_x, bc2_x, h_ways), (a2_y, bc2_y, h_ways)))

    def arrived(ref, sem):
        remote(ref, ref, sem, sem, sibling).wait_recv()

    def x1(kind, i):
        step, cols = ((2, low_x), (2, high_x), (1, high_x), (3, low_x), (0, None), (0, None))[kind]
        source = p16_x.at[i, rows(x, step, 64), cols] if kind < 4 else c1_x.at[kind - 4, i]
        return message(0, 0, kind, i, source)

    def y1(kind, i):
        step, cols = ((2, low_y), (2, high_y), (1, high_y), (3, low_y), (0, None), (0, None))[kind]
        source = p16_y.at[i, step, :, :, :, cols] if kind < 4 else c1_y.at[kind - 4, i]
        return message(0, 1, kind, i, source)

    def mine(step):
        return pl.ds(pl.multiple_of(x * 64 + lax.rem(hi + step, 4) * 16, 16), 16)

    def x2(kind, i):
        step, cols = ((2, low_x), (2, high_x), (1, high_x), (3, low_x), (0, None), (0, None))[kind]
        source = p16_x.at[i, mine(step), cols] if kind < 4 else c2_x.at[kind - 4, i]
        return message(1, 0, kind, i, source)

    def y2(kind, i):
        step, cols = ((2, low_y), (2, high_y), (1, high_y), (3, low_y), (0, None), (0, None))[kind]
        source = p16_y.at[i, 0, :, lax.rem(hi + step, 4), :, cols] if kind < 4 else c2_y.at[kind - 4, i]
        return message(1, 1, kind, i, source)

    def line_message(i):
        d = lax.rem(4 - roles[i], 4)
        return remote(t16_x.at[i], line.at[d], send_sem.at[2, 0, 0], last_recv.at[0], {"y": blocks[i]})

    def plane_message(i, e):
        d = lax.rem(4 - roles[i], 4)
        to = lax.rem(x + e, 4)
        n = 1 if e else 0
        return remote(
            t16_y.at[i, to], plane.at[d, (4 - e) % 4], send_sem.at[2, 1, n], last_recv.at[1 + n],
            {"y": blocks[i], "x": to},
        )

    def x_product(i, first=False):
        with scope(f"x_product{i}"):
            for half in range(2):

                def step(j, carry):
                    j = half * (HX // TILE) + j
                    if first:
                        get_w(j).wait()
                    cols = pl.ds(pl.multiple_of(j * TILE, TILE), TILE)
                    part = jnp.dot(h[i], w_v[:, cols], preferred_element_type=F32)
                    p32_x[i, :, cols] = part
                    p16_x[i, :, cols] = part.astype(BF16)
                    return carry

                lax.fori_loop(0, HX // TILE, step, 0)
                for kind in ((0, 3), (1, 2))[half]:
                    x1(kind, i).start()

    def y_product(i, first=False):
        with scope(f"y_product{i}"):

            def quarter(r):
                at = lax.rem(y + r, 4)
                if first:
                    get_w(WX // TILE + at).wait()
                cols = pl.ds(pl.multiple_of(WX + at * QY, QY), QY)
                part = jnp.dot(h[i], w_v[:, cols], preferred_element_type=F32).reshape(4, 4, 16, QY)
                p32_y[i, r] = part
                p16_y[i, r] = part.astype(BF16)

            quarter(2)
            for kind in (0, 1):
                y1(kind, i).start()
            lax.fori_loop(0, 3, lambda j, c: (quarter(lax.rem(5 - j, 4)), c)[1], 0)
            for kind in (2, 3):
                y1(kind, i).start()

    def x_relay(i):
        with scope(f"x_relay{i}"):
            for s, step in ((0, 1), (1, 3)):
                arrived(a1_x.at[s, i], a1_recv.at[0, s, i])
                own = p32_x[i, rows(x, step, 64), s * HX : (s + 1) * HX]
                c1_x[s, i] = (own + a1_x[s, i].astype(F32)).astype(BF16)
                x1(4 + s, i).start()

    def y_relay(i):
        with scope(f"y_relay{i}"):
            for s, r in ((0, 1), (1, 3)):
                arrived(a1_y.at[s, i], a1_recv.at[1, s, i])
                own = p32_y[i, r, :, :, :, s * HY : (s + 1) * HY]
                c1_y[s, i] = (own + a1_y[s, i].astype(F32)).astype(BF16)
                y1(4 + s, i).start()

    halves = ((2, 1), (0, 3))

    def x_finish(i):
        with scope(f"x_finish{i}"):
            arrived(bc1_x.at[i], bc1_recv.at[0, i])
            own = rows(x, 0, 64)
            for s, (a, b) in enumerate(halves):
                cols = pl.ds(s * HX, HX)
                total = p32_x[i, own, cols] + bc1_x[i, a].astype(F32) + bc1_x[i, b].astype(F32)
                p32_x[i, own, cols] = total
                p16_x[i, own, cols] = total.astype(BF16)
            for kind in (0, 1, 2, 3):
                x2(kind, i).start()

    def y_finish(i):
        with scope(f"y_finish{i}"):
            arrived(bc1_y.at[i], bc1_recv.at[1, i])
            for s, (a, b) in enumerate(halves):
                cols = pl.ds(s * HY, HY)
                total = p32_y[i, 0, :, :, :, cols] + bc1_y[i, a].astype(F32) + bc1_y[i, b].astype(F32)
                p32_y[i, 0, :, :, :, cols] = total
                p16_y[i, 0, :, :, :, cols] = total.astype(BF16)
            for kind in (0, 1, 2, 3):
                y2(kind, i).start()

    def x_relay2(i):
        with scope(f"x_second{i}"):
            for s, step in ((0, 1), (1, 3)):
                arrived(a2_x.at[s, i], a2_recv.at[0, s, i])
                own = p32_x[i, mine(step), s * HX : (s + 1) * HX]
                c2_x[s, i] = (own + a2_x[s, i].astype(F32)).astype(BF16)
                x2(4 + s, i).start()

    def y_relay2(i):
        with scope(f"y_second{i}"):
            for s, step in ((0, 1), (1, 3)):
                arrived(a2_y.at[s, i], a2_recv.at[1, s, i])
                own = p32_y[i, 0, :, lax.rem(hi + step, 4), :, s * HY : (s + 1) * HY]
                c2_y[s, i] = (own + a2_y[s, i].astype(F32)).astype(BF16)
                y2(4 + s, i).start()

    def x_finish2(i):
        with scope(f"x_finish_second{i}"):
            arrived(bc2_x.at[i], bc2_recv.at[0, i])
            for s, (a, b) in enumerate(halves):
                cols = pl.ds(s * HX, HX)
                total = p32_x[i, mine(0), cols] + bc2_x[i, a].astype(F32) + bc2_x[i, b].astype(F32)
                t32_x[i, :, cols] = total
                t16_x[i, :, cols] = total.astype(LAST_X)

            @pl.when(roles[i] != 0)
            def _():
                line_message(i).start()

    def y_finish2(i):
        with scope(f"y_finish_second{i}"):
            arrived(bc2_y.at[i], bc2_recv.at[1, i])
            for s, (a, b) in enumerate(halves):
                cols = pl.ds(s * HY, HY)
                total = p32_y[i, 0, :, hi, :, cols] + bc2_y[i, a].astype(F32) + bc2_y[i, b].astype(F32)
                t32_y[i, :, :, cols] = total
                t16_y[i, :, :, cols] = total.astype(LAST_Y)
            for e in (2, 1, 3):
                plane_message(i, e).start()

            @pl.when(roles[i] != 0)
            def _():
                plane_message(i, 0).start()

    def folded(value):
        total = value[:, :128]
        for j in range(1, value.shape[1] // 128):
            total = total + value[:, j * 128 : (j + 1) * 128]
        return total

    def close(total, cols, squares):
        total = total + res_ref[:, cols].astype(F32)
        summed[:, cols] = total
        out_ref[0, :, cols] = total.astype(BF16)
        return squares + folded(total * total)

    def x_close(squares):
        with scope("x_close"):
            arrived(line.at[pl.ds(1, 3)], last_recv.at[0])
            total = t32_x[own_slot]
            for d in (1, 2, 3):
                total = total + line[d].astype(F32)
            return close(total, pl.ds(0, WX), squares)

    def y_close(squares):
        with scope("y_close"):
            arrived(plane.at[pl.ds(1, 3), 0], last_recv.at[1])
            arrived(plane.at[:, pl.ds(1, 3)], last_recv.at[2])
            for d in range(4):
                total = plane[d, 0].astype(F32) if d else t32_y[own_slot, x]
                for e in (1, 2, 3):
                    total = total + plane[d, e].astype(F32)
                squares = close(total, pl.ds(pl.multiple_of(WX + lax.rem(y + d, 4) * QY, QY), QY), squares)
            return squares

    own_slot = 2 * lax.rem(y // 2 + lo, 2) + lax.rem(y + core, 2)
    y_product(0, first=True)
    x_product(0, first=True)
    y_relay(0)
    with scope("gather0"):
        gathers[0].wait_recv()
    y_product(1)
    x_relay(0)
    x_product(1)
    y_finish(0)
    x_finish(0)
    y_relay(1)
    with scope("gather1"):
        gathers[1].wait_recv()
    gathers[2].start()
    y_product(2)
    x_relay(1)
    with scope("gather2"):
        gathers[2].wait_recv()
    x_product(3)
    x_relay2(0)
    y_finish(1)
    x_finish(1)
    y_relay(2)
    y_relay2(0)
    y_product(3)
    y_relay2(1)
    x_relay(3)
    x_relay2(1)
    x_product(2)
    x_finish(3)
    y_finish(2)
    y_relay(3)
    x_finish2(1)
    x_relay2(3)
    x_relay(2)
    y_finish(3)
    x_finish2(0)
    x_finish(2)
    y_finish2(0)
    y_relay2(3)
    y_relay2(2)
    y_finish2(1)
    x_finish2(3)
    x_relay2(2)
    y_finish2(3)
    y_finish2(2)
    x_finish2(2)
    for copy in get_rest:
        copy.wait()
    total = y_close(x_close(jnp.zeros((16, 128), F32)))

    sq_own[...] = total
    exchange = [
        remote(sq_own, sq_in.at[i], n_sem.at[0], n_sem.at[1], who)
        for i, who in enumerate((sibling, across, diagonal))
    ]
    for copy in exchange:
        copy.start()
    with scope("drain"):
        arrived(h.at[pl.ds(0, 3)], ag_send)
        for colour, (bc1, c1, bc2, c2) in enumerate(((bc1_x, c1_x, bc2_x, c2_x), (bc1_y, c1_y, bc2_y, c2_y))):
            for stage, bc, c in ((0, bc1, c1), (1, bc2, c2)):
                arrived(bc, send_sem.at[stage, colour, 0])
                arrived(c, send_sem.at[stage, colour, 1])
        arrived(line.at[pl.ds(1, 3)], send_sem.at[2, 0, 0])
        arrived(plane.at[pl.ds(1, 3), 0], send_sem.at[2, 1, 0])
        arrived(plane.at[:, pl.ds(1, 3)], send_sem.at[2, 1, 1])

    with scope("exchange"):
        arrived(sq_in, n_sem.at[1])
    for i in range(3):
        total = total + sq_in[i]
    with scope("norm"):
        scale = lax.rsqrt(jnp.sum(total, axis=1, keepdims=True) / D + 1e-05)
        for j in range(N // 128):
            cols = pl.ds(j * 128, 128)
            out_ref[1, :, cols] = (summed[:, cols] * scale * gain_ref[j : j + 1, :].astype(F32)).astype(BF16)
    arrived(sq_in, n_sem.at[0])


def body(gate_in, up_in, down_weight, residual, norm_gain):
    dma = pltpu.SemaphoreType.DMA
    vm = pltpu.VMEM
    scratch = [vm((K, 256), BF16), vm((K, 256), BF16), vm((16, N), BF16), vm((N // 128, 128), BF16), vm((KP, N), BF16), vm((4, 256, KP), BF16)]
    scratch += [vm((4, 256, WX), F32), vm((4, 256, WX), BF16)]
    scratch += [vm((4, 4, 4, 4, 16, QY), F32), vm((4, 4, 4, 4, 16, QY), BF16)]
    for rows, cols in (((64,), HX), ((4, 4, 16), HY), ((16,), HX), ((4, 16), HY)):
        scratch += [vm((2, 4, *rows, cols), BF16), vm((4, 4, *rows, cols), BF16), vm((2, 4, *rows, cols), BF16)]
    scratch += [vm((4, 16, WX), F32), vm((4, 16, WX), LAST_X), vm((4, 4, 16, QY), F32), vm((4, 4, 16, QY), LAST_Y)]
    scratch += [vm((4, 16, WX), LAST_X), vm((4, 4, 16, QY), LAST_Y)]
    scratch += [vm((16, N), F32), vm((16, 128), F32), vm((3, 16, 128), F32)]
    scratch += [dma((4,)), dma((N // TILE,)), dma, dma((3,)), dma((3, 2, 2))]
    scratch += [dma((2, 2, 4)), dma((2, 4)), dma((2, 2, 4)), dma((2, 4)), dma((3,)), dma((2,))]
    anywhere = pl.BlockSpec(memory_space=pltpu.HBM)
    vmem = pl.BlockSpec(memory_space=pltpu.VMEM)
    both = pl.pallas_call(
        kernel,
        out_shape=jax.ShapeDtypeStruct((2, 16, N), BF16),
        in_specs=[anywhere] * 5,
        out_specs=vmem,
        scratch_shapes=scratch,
        compiler_params=pltpu.CompilerParams(
            collective_id=0, has_side_effects=True, vmem_limit_bytes=VMEM_LIMIT
        ),
    )(gate_in.T, up_in.T, down_weight, residual, norm_gain.reshape(N // 128, 128))
    return both[0], both[1]


def solution(mesh):
    split = Mesh(mesh.devices.reshape(4, 4, 4, 2, 2), ("y", "x", "h", "l", "c"))
    tp, col = ("y", "x", "h"), ("l", "c")
    return jax.shard_map(
        body,
        mesh=split,
        in_specs=(P(col, tp), P(col, tp), P(tp, col), P(tp, col), P(col)),
        out_specs=(P(tp, col), P(tp, col)),
        check_vma=False,
    )
```

time: 303 us -> 77 us (0.25)
  waiting for transfers between devices: 237 us -> 0 us
  Pallas kernels: 0 us -> 74.5 us
  blocking collectives: 33.2 us -> 0 us
  between operations: 14.5 us -> 0.64 us
  matrix products: 11.6 us -> 0 us
  other arithmetic: 4.24 us -> 0 us
    reduce_scatter x3 -> x0, waiting for transfers between devices: 237 us -> none  [summed_rows(): nearer = lax.psum_scatter(value, axes[0], scatter_dimension=dim, tiled=True)]
    pallas_call x0 -> x1, Pallas kernels: none -> 74.5 us  [body(): pl.pallas_call(kernel, out_shape=jax.ShapeDtypeStruct((2, 16, N), BF16),...]
    all_to_all x1 -> x0, blocking collectives: 26.5 us -> none  [from_everyone(): lax.all_to_all(jnp.broadcast_to(value[None], (peers, *value.shape)), axis...]
    dot_general x1 -> x0, matrix products: 11.6 us -> none  [body(): jnp.dot(hidden, down_weight, preferred_element_type=jnp.float32)]
    unnamed x1 -> x0, blocking collectives: 6.78 us -> none
    convert_element_type x3 -> x0, other arithmetic: 3.12 us -> none  [the longest x1 1.7 us: body(): return (summed.astype(jnp.bfloat16), scaled.astype(jnp.bfloat16))]
  transfers between devices with their start and end apart: 3 -> 0, of which waited for: 3 -> 0; matrix products, arithmetic and copies ran while one was open for 0% -> 0% of each run, Pallas kernels for 0% -> 0%
where the time goes in v3:
time: 77 us; the launch traced here: 76.8 us
  Pallas kernels  74.5 us (97%)
  local copies, waits for them, and re-layouts  1.68 us (2%)
    pallas_call x1, Pallas kernels, body(): pl.pallas_call(kernel, out_shape=jax.ShapeDtypeStruct((2, 16, N), BF16),...  74.5 us
    squeeze x1, local copies, waits for them, and re-layouts, body(): return (both[0], both[1])  1.68 us

profile of v3, /device:TPU:1, one launch (start us, length us, event | category | flops | bytes accessed | tf_op | source)
XLA Modules:
  0.0 76.8 jit_solution(16033305822533355449)
XLA Ops:
  0.6 74.5 %shard_map.68 = bf16[2,16,4096]{2,1,0:T(8,128)(2,1)} custom-call(bf16[832,256]{1,0:T(8,128)(2,1)} %bitcast.7, bf16[832,256]{1,0:T(8,128)(2,1)} %bitcast.8, bf16[832,4096]{1,0:T(8,128)(2,1)} %w_hbm.1, bf16[16,4096]{1,0:T(8,128)(2,1)} %res_hbm.1, bf16[32,128]{1,0:T(8,128)(2,1)} %bitcast.9), custom_call_target="tpu_custom_call" | custom-call | tf_op jit(solution)/shard_map/pallas_call | solution.py:416
  75.1 1.7 %slice_bitcast_fusion = (bf16[16,4096]{1,0:T(8,128)(2,1)}, bf16[16,4096]{1,0:T(8,128)(2,1)}) fusion(bf16[2,16,4096]{2,1,0:T(8,128)(2,1)} %shard_map.68), kind=kLoop, calls=%fused_computation | loop fusion | bytes 524288 | tf_op jit(solution)/shard_map/squeeze | solution.py:426

commit v4 on v3

--- a/solution.py
+++ b/solution.py
@@ -15,7 +15,7 @@
 K = 832
 KP = 896
 TILE = 512
-VMEM_LIMIT = 58 * 1024 * 1024
+VMEM_LIMIT = 50 * 1024 * 1024
 WX = 2048
 WY = N - WX
 HX, QY = WX // 2, WY // 4
@@ -164,40 +164,59 @@
             {"y": blocks[i], "x": to},
         )
 
-    def x_product(i, first=False):
+    def x_half(i, half):
+        def step(j, carry):
+            j = half * (HX // TILE) + j
+            if i == 0:
+                get_w(j).wait()
+            cols = pl.ds(pl.multiple_of(j * TILE, TILE), TILE)
+            part = jnp.dot(h[i], w_v[:, cols], preferred_element_type=F32)
+            p32_x[i, :, cols] = part
+            p16_x[i, :, cols] = part.astype(BF16)
+            return carry
+
+        lax.fori_loop(0, HX // TILE, step, 0)
+
+    def y_quarters(i, count):
+        def step(j, carry):
+            r = lax.rem(5 - j, 4) if count == 3 else 2
+            at = lax.rem(y + r, 4)
+            if i == 0:
+                get_w(WX // TILE + at).wait()
+            cols = pl.ds(pl.multiple_of(WX + at * QY, QY), QY)
+            part = jnp.dot(h[i], w_v[:, cols], preferred_element_type=F32).reshape(4, 4, 16, QY)
+            p32_y[i, r] = part
+            p16_y[i, r] = part.astype(BF16)
+            return carry
+
+        lax.fori_loop(0, count, step, 0)
+
+    def first_product():
+        with scope("first_product"):
+            y_quarters(0, 1)
+            for kind in (0, 1):
+                y1(kind, 0).start()
+            for half, kinds in enumerate(((0, 3), (1, 2))):
+                x_half(0, half)
+                for kind in kinds:
+                    x1(kind, 0).start()
+            y_quarters(0, 3)
+            for kind in (2, 3):
+                y1(kind, 0).start()
+
+    def x_product(i):
         with scope(f"x_product{i}"):
-            for half in range(2):
-
-                def step(j, carry):
-                    j = half * (HX // TILE) + j
-                    if first:
-                        get_w(j).wait()
-                    cols = pl.ds(pl.multiple_of(j * TILE, TILE), TILE)
-                    part = jnp.dot(h[i], w_v[:, cols], preferred_element_type=F32)
-                    p32_x[i, :, cols] = part
-                    p16_x[i, :, cols] = part.astype(BF16)
-                    return carry
-
-                lax.fori_loop(0, HX // TILE, step, 0)
-                for kind in ((0, 3), (1, 2))[half]:
-                    x1(kind, i).start()
-
-    def y_product(i, first=False):
+            x_half(i, 0)
+            x_half(i, 1)
+            for kind in (0, 1, 2, 3):
+                x1(kind, i).start()
+
+    def y_product(i):
         with scope(f"y_product{i}"):
-
-            def quarter(r):
-                at = lax.rem(y + r, 4)
-                if first:
-                    get_w(WX // TILE + at).wait()
-                cols = pl.ds(pl.multiple_of(WX + at * QY, QY), QY)
-                part = jnp.dot(h[i], w_v[:, cols], preferred_element_type=F32).reshape(4, 4, 16, QY)
-                p32_y[i, r] = part
-                p16_y[i, r] = part.astype(BF16)
-
-            quarter(2)
+            y_quarters(i, 1)
             for kind in (0, 1):
                 y1(kind, i).start()
-            lax.fori_loop(0, 3, lambda j, c: (quarter(lax.rem(5 - j, 4)), c)[1], 0)
+            y_quarters(i, 3)
             for kind in (2, 3):
                 y1(kind, i).start()
 
@@ -318,8 +337,7 @@
             return squares
 
     own_slot = 2 * lax.rem(y // 2 + lo, 2) + lax.rem(y + core, 2)
-    y_product(0, first=True)
-    x_product(0, first=True)
+    first_product()
     y_relay(0)
     with scope("gather0"):
         gathers[0].wait_recv()
@@ -334,6 +352,7 @@
     gathers[2].start()
     y_product(2)
     x_relay(1)
+    y_relay2(0)
     with scope("gather2"):
         gathers[2].wait_recv()
     x_product(3)
@@ -341,29 +360,28 @@
     y_finish(1)
     x_finish(1)
     y_relay(2)
-    y_relay2(0)
     y_product(3)
     y_relay2(1)
     x_relay(3)
+    x_product(2)
     x_relay2(1)
-    x_product(2)
+    y_finish(2)
     x_finish(3)
-    y_finish(2)
     y_relay(3)
+    x_finish2(0)
+    y_relay2(2)
+    y_finish2(1)
+    x_relay(2)
     x_finish2(1)
     x_relay2(3)
-    x_relay(2)
     y_finish(3)
-    x_finish2(0)
     x_finish(2)
+    y_relay2(3)
     y_finish2(0)
-    y_relay2(3)
-    y_relay2(2)
-    y_finish2(1)
+    y_finish2(2)
+    x_relay2(2)
     x_finish2(3)
-    x_relay2(2)
     y_finish2(3)
-    y_finish2(2)
     x_finish2(2)
     for copy in get_rest:
         copy.wait()
@@ -413,6 +431,8 @@
     scratch += [dma((2, 2, 4)), dma((2, 4)), dma((2, 2, 4)), dma((2, 4)), dma((3,)), dma((2,))]
     anywhere = pl.BlockSpec(memory_space=pltpu.HBM)
     vmem = pl.BlockSpec(memory_space=pltpu.VMEM)
+    operands = (gate_in.T, up_in.T, down_weight, residual, norm_gain.reshape(N // 128, 128))
+    operands = (pltpu.with_memory_space_constraint(a, pltpu.HBM) for a in operands)
     both = pl.pallas_call(
         kernel,
         out_shape=jax.ShapeDtypeStruct((2, 16, N), BF16),
@@ -422,7 +442,7 @@
         compiler_params=pltpu.CompilerParams(
             collective_id=0, has_side_effects=True, vmem_limit_bytes=VMEM_LIMIT
         ),
-    )(gate_in.T, up_in.T, down_weight, residual, norm_gain.reshape(N // 128, 128))
+    )(*operands)
     return both[0], both[1]
 
 

time: 77 us -> 71.1 us (0.923)
  Pallas kernels: 74.5 us -> 69.6 us
  local copies, waits for them, and re-layouts: 1.68 us -> 0.72 us
    pallas_call x1, Pallas kernels: 74.5 us -> 69.6 us  [body(): pl.pallas_call(kernel, out_shape=jax.ShapeDtypeStruct((2, 16, N), BF16),...]
    squeeze x1, local copies, waits for them, and re-layouts: 1.68 us -> 0.72 us  [body(): return (both[0], both[1])]
where the time goes in v4:
time: 71.1 us; the launch traced here: 71 us
  Pallas kernels  69.6 us (98%)
  local copies, waits for them, and re-layouts  0.72 us (1%)
    pallas_call x1, Pallas kernels, body(): pl.pallas_call(kernel, out_shape=jax.ShapeDtypeStruct((2, 16, N), BF16),...  69.6 us

profile of v4, /device:TPU:1, one launch (start us, length us, event | category | flops | bytes accessed | tf_op | source)
XLA Modules:
  0.0 71.0 jit_solution(15881204096973814948)
XLA Ops:
  0.6 69.6 %shard_map.68 = bf16[2,16,4096]{2,1,0:T(8,128)(2,1)S(1)} custom-call(bf16[832,256]{1,0:T(8,128)(2,1)} %bitcast.7, bf16[832,256]{1,0:T(8,128)(2,1)} %bitcast.8, bf16[832,4096]{1,0:T(8,128)(2,1)} %w_hbm.1, bf16[16,4096]{1,0:T(8,128)(2,1)} %res_hbm.1, bf16[32,128]{1,0:T(8,128)(2,1)} %bitcast.9), custom_call_target="tpu_custom_call" | custom-call | tf_op jit(solution)/shard_map/pallas_call | solution.py:436
  70.2 0.7 %slice_bitcast_fusion = (bf16[16,4096]{1,0:T(8,128)(2,1)}, bf16[16,4096]{1,0:T(8,128)(2,1)}) fusion(bf16[2,16,4096]{2,1,0:T(8,128)(2,1)S(1)} %shard_map.68), kind=kLoop, calls=%fused_computation | loop fusion | bytes 524288 | tf_op jit(solution)/shard_map/squeeze | solution.py:446

commit v5 on v4

--- a/solution.py
+++ b/solution.py
@@ -21,7 +21,7 @@
 HX, QY = WX // 2, WY // 4
 HY = QY // 2
 LAST_X = BF16
-LAST_Y = F32
+LAST_Y = BF16
 
 
 def kernel(
@@ -61,13 +61,14 @@
     for who in partners:
         pl.semaphore_signal(barrier, inc=1, device_id=who, device_id_type=pl.DeviceIdType.MESH)
 
-    for j in range(HX // TILE):
+    y_tile = WX // TILE
+    for j in (y_tile + lax.rem(y + 2, 4), *range(HX // TILE)):
         get_w(j).start()
     w_v[K:, :] = jnp.zeros((KP - K, N), BF16)
     with scope("get_in"):
         get_gate.wait()
         get_up.wait()
-    for j in range(HX // TILE, N // TILE):
+    for j in (*range(HX // TILE, y_tile), *(y_tile + lax.rem(y + r, 4) for r in (1, 0, 3))):
         get_w(j).start()
     get_rest = [
         pltpu.make_async_copy(res_hbm, res_ref, in_sem.at[2]),
@@ -85,9 +86,6 @@
             act = jnp.concatenate([act, jnp.zeros((128 - depth, 256), F32)], axis=0)
         h[0, :, k * 128 : (k + 1) * 128] = act.T.astype(BF16)
 
-    with scope("barrier"):
-        pl.semaphore_wait(barrier, len(partners))
-
     def remote(src, dst, send, recv, who):
         return pltpu.make_async_remote_copy(
             src_ref=src, dst_ref=dst, send_sem=send, recv_sem=recv,
@@ -99,9 +97,6 @@
         remote(h.at[0], h.at[2], ag_send, ag_recv.at[1], across),
         remote(h.at[2], h.at[3], ag_send, ag_recv.at[2], sibling),
     ]
-    gathers[1].start()
-    gathers[0].start()
-
     blocks = (2 * lo + core, 2 * lo + 1 - core, 2 * (1 - lo) + core, 2 * (1 - lo) + 1 - core)
     roles = [lax.rem(b + 4 - y, 4) for b in blocks]
 
@@ -194,12 +189,18 @@
     def first_product():
         with scope("first_product"):
             y_quarters(0, 1)
+            x_half(0, 0)
+            with scope("barrier"):
+                pl.semaphore_wait(barrier, len(partners))
+            gathers[1].start()
+            gathers[0].start()
             for kind in (0, 1):
                 y1(kind, 0).start()
-            for half, kinds in enumerate(((0, 3), (1, 2))):
-                x_half(0, half)
-                for kind in kinds:
-                    x1(kind, 0).start()
+            for kind in (0, 3):
+                x1(kind, 0).start()
+            x_half(0, 1)
+            for kind in (1, 2):
+                x1(kind, 0).start()
             y_quarters(0, 3)
             for kind in (2, 3):
                 y1(kind, 0).start()
@@ -208,7 +209,7 @@
         with scope(f"x_product{i}"):
             x_half(i, 0)
             x_half(i, 1)
-            for kind in (0, 1, 2, 3):
+            for kind in (0, 1):
                 x1(kind, i).start()
 
     def y_product(i):
@@ -217,8 +218,14 @@
             for kind in (0, 1):
                 y1(kind, i).start()
             y_quarters(i, 3)
-            for kind in (2, 3):
-                y1(kind, i).start()
+
+    def x_direct(i):
+        for kind in (2, 3):
+            x1(kind, i).start()
+
+    def y_direct(i):
+        for kind in (2, 3):
+            y1(kind, i).start()
 
     def x_relay(i):
         with scope(f"x_relay{i}"):
@@ -342,8 +349,10 @@
     with scope("gather0"):
         gathers[0].wait_recv()
     y_product(1)
+    y_direct(1)
     x_relay(0)
     x_product(1)
+    x_direct(1)
     y_finish(0)
     x_finish(0)
     y_relay(1)
@@ -351,19 +360,23 @@
         gathers[1].wait_recv()
     gathers[2].start()
     y_product(2)
+    y_direct(2)
     x_relay(1)
     y_relay2(0)
     with scope("gather2"):
         gathers[2].wait_recv()
     x_product(3)
+    x_direct(3)
     x_relay2(0)
     y_finish(1)
     x_finish(1)
     y_relay(2)
     y_product(3)
+    y_direct(3)
     y_relay2(1)
     x_relay(3)
     x_product(2)
+    x_direct(2)
     x_relay2(1)
     y_finish(2)
     x_finish(3)

time: 71.1 us -> 70.1 us (0.986)
  Pallas kernels: 69.6 us -> 68.6 us
    pallas_call x1, Pallas kernels: 69.6 us -> 68.6 us  [body(): pl.pallas_call(kernel, out_shape=jax.ShapeDtypeStruct((2, 16, N), BF16),...]
where the time goes in v5:
time: 70.1 us; the launch traced here: 70 us
  Pallas kernels  68.6 us (98%)
  local copies, waits for them, and re-layouts  0.72 us (1%)
    pallas_call x1, Pallas kernels, body(): pl.pallas_call(kernel, out_shape=jax.ShapeDtypeStruct((2, 16, N), BF16),...  68.6 us

profile of v5, /device:TPU:1, one launch (start us, length us, event | category | flops | bytes accessed | tf_op | source)
XLA Modules:
  0.0 70.0 jit_solution(7595198984921744790)
XLA Ops:
  0.6 68.6 %shard_map.68 = bf16[2,16,4096]{2,1,0:T(8,128)(2,1)S(1)} custom-call(bf16[832,256]{1,0:T(8,128)(2,1)} %bitcast.7, bf16[832,256]{1,0:T(8,128)(2,1)} %bitcast.8, bf16[832,4096]{1,0:T(8,128)(2,1)} %w_hbm.1, bf16[16,4096]{1,0:T(8,128)(2,1)} %res_hbm.1, bf16[32,128]{1,0:T(8,128)(2,1)} %bitcast.9), custom_call_target="tpu_custom_call" | custom-call | tf_op jit(solution)/shard_map/pallas_call | solution.py:449
  69.3 0.7 %slice_bitcast_fusion = (bf16[16,4096]{1,0:T(8,128)(2,1)}, bf16[16,4096]{1,0:T(8,128)(2,1)}) fusion(bf16[2,16,4096]{2,1,0:T(8,128)(2,1)S(1)} %shard_map.68), kind=kLoop, calls=%fused_computation | loop fusion | bytes 524288 | tf_op jit(solution)/shard_map/squeeze | solution.py:459

commit v6 on v5

--- a/solution.py
+++ b/solution.py
@@ -170,7 +170,7 @@
             p16_x[i, :, cols] = part.astype(BF16)
             return carry
 
-        lax.fori_loop(0, HX // TILE, step, 0)
+        lax.fori_loop(0, HX // TILE, step, 0, unroll=True)
 
     def y_quarters(i, count):
         def step(j, carry):
@@ -184,7 +184,7 @@
             p16_y[i, r] = part.astype(BF16)
             return carry
 
-        lax.fori_loop(0, count, step, 0)
+        lax.fori_loop(0, count, step, 0, unroll=True)
 
     def first_product():
         with scope("first_product"):
@@ -345,57 +345,57 @@
 
     own_slot = 2 * lax.rem(y // 2 + lo, 2) + lax.rem(y + core, 2)
     first_product()
-    y_relay(0)
     with scope("gather0"):
         gathers[0].wait_recv()
+    x_product(1)
+    y_relay(0)
+    x_relay(0)
     y_product(1)
+    x_direct(1)
     y_direct(1)
-    x_relay(0)
-    x_product(1)
-    x_direct(1)
     y_finish(0)
+    x_relay(1)
     x_finish(0)
-    y_relay(1)
     with scope("gather1"):
         gathers[1].wait_recv()
     gathers[2].start()
+    y_relay(1)
+    x_product(2)
+    y_relay2(0)
     y_product(2)
     y_direct(2)
-    x_relay(1)
-    y_relay2(0)
+    x_relay2(0)
+    y_finish(1)
+    x_direct(2)
     with scope("gather2"):
         gathers[2].wait_recv()
     x_product(3)
-    x_direct(3)
-    x_relay2(0)
-    y_finish(1)
     x_finish(1)
     y_relay(2)
     y_product(3)
+    y_relay2(1)
+    x_relay(2)
     y_direct(3)
-    y_relay2(1)
-    x_relay(3)
-    x_product(2)
-    x_direct(2)
     x_relay2(1)
     y_finish(2)
+    y_relay(3)
+    x_direct(3)
+    x_finish(2)
+    y_finish2(0)
+    x_relay(3)
+    y_relay2(2)
+    x_finish2(0)
+    x_relay2(2)
+    y_finish(3)
+    y_finish2(2)
     x_finish(3)
-    y_relay(3)
-    x_finish2(0)
-    y_relay2(2)
+    x_finish2(2)
+    y_relay2(3)
     y_finish2(1)
-    x_relay(2)
+    x_relay2(3)
+    y_finish2(3)
     x_finish2(1)
-    x_relay2(3)
-    y_finish(3)
-    x_finish(2)
-    y_relay2(3)
-    y_finish2(0)
-    y_finish2(2)
-    x_relay2(2)
     x_finish2(3)
-    y_finish2(3)
-    x_finish2(2)
     for copy in get_rest:
         copy.wait()
     total = y_close(x_close(jnp.zeros((16, 128), F32)))

time: 70.1 us -> 68.2 us (0.973)
  the two profiles are of different devices: /device:TPU:1 before, /device:TPU:9 now
where the time goes in v6:
time: 68.2 us; the launch traced here: 68.1 us
  Pallas kernels  66.8 us (98%)
  local copies, waits for them, and re-layouts  0.72 us (1%)
    pallas_call x1, Pallas kernels, body(): pl.pallas_call(kernel, out_shape=jax.ShapeDtypeStruct((2, 16, N), BF16),...  66.8 us

profile of v6, /device:TPU:9, one launch (start us, length us, event | category | flops | bytes accessed | tf_op | source)
XLA Modules:
  0.0 68.1 jit_solution(5907269113602101417)
XLA Ops:
  0.6 66.8 %shard_map.68 = bf16[2,16,4096]{2,1,0:T(8,128)(2,1)S(1)} custom-call(bf16[832,256]{1,0:T(8,128)(2,1)} %bitcast.7, bf16[832,256]{1,0:T(8,128)(2,1)} %bitcast.8, bf16[832,4096]{1,0:T(8,128)(2,1)} %w_hbm.1, bf16[16,4096]{1,0:T(8,128)(2,1)} %res_hbm.1, bf16[32,128]{1,0:T(8,128)(2,1)} %bitcast.9), custom_call_target="tpu_custom_call" | custom-call | tf_op jit(solution)/shard_map/pallas_call | solution.py:449
  67.4 0.7 %slice_bitcast_fusion = (bf16[16,4096]{1,0:T(8,128)(2,1)}, bf16[16,4096]{1,0:T(8,128)(2,1)}) fusion(bf16[2,16,4096]{2,1,0:T(8,128)(2,1)S(1)} %shard_map.68), kind=kLoop, calls=%fused_computation | loop fusion | bytes 524288 | tf_op jit(solution)/shard_map/squeeze | solution.py:459

commit v7 on v6

--- a/solution.py
+++ b/solution.py
@@ -190,16 +190,14 @@
         with scope("first_product"):
             y_quarters(0, 1)
             x_half(0, 0)
+            x_half(0, 1)
             with scope("barrier"):
                 pl.semaphore_wait(barrier, len(partners))
             gathers[1].start()
             gathers[0].start()
             for kind in (0, 1):
                 y1(kind, 0).start()
-            for kind in (0, 3):
-                x1(kind, 0).start()
-            x_half(0, 1)
-            for kind in (1, 2):
+            for kind in (0, 1, 2, 3):
                 x1(kind, 0).start()
             y_quarters(0, 3)
             for kind in (2, 3):

time: 68.2 us -> 68.8 us (level)
  no operation moved by 1% of the time
where the time goes in v7:
time: 68.8 us; the launch traced here: 68.7 us
  Pallas kernels  67.4 us (98%)
  local copies, waits for them, and re-layouts  0.72 us (1%)
    pallas_call x1, Pallas kernels, body(): pl.pallas_call(kernel, out_shape=jax.ShapeDtypeStruct((2, 16, N), BF16),...  67.4 us

profile of v7, /device:TPU:9, one launch (start us, length us, event | category | flops | bytes accessed | tf_op | source)
XLA Modules:
  0.0 68.7 jit_solution(15440398414605197543)
XLA Ops:
  0.6 67.4 %shard_map.68 = bf16[2,16,4096]{2,1,0:T(8,128)(2,1)S(1)} custom-call(bf16[832,256]{1,0:T(8,128)(2,1)} %bitcast.7, bf16[832,256]{1,0:T(8,128)(2,1)} %bitcast.8, bf16[832,4096]{1,0:T(8,128)(2,1)} %w_hbm.1, bf16[16,4096]{1,0:T(8,128)(2,1)} %res_hbm.1, bf16[32,128]{1,0:T(8,128)(2,1)} %bitcast.9), custom_call_target="tpu_custom_call" | custom-call | tf_op jit(solution)/shard_map/pallas_call | solution.py:447
  68.0 0.7 %slice_bitcast_fusion = (bf16[16,4096]{1,0:T(8,128)(2,1)}, bf16[16,4096]{1,0:T(8,128)(2,1)}) fusion(bf16[2,16,4096]{2,1,0:T(8,128)(2,1)S(1)} %shard_map.68), kind=kLoop, calls=%fused_computation | loop fusion | bytes 524288 | tf_op jit(solution)/shard_map/squeeze | solution.py:457
